TPU v7x, 128 devices: a whole 4x4x4 slice. The times are simulated.
128 devices in a mesh: row: 16 (over y, z), col: 8 (over x, core).
Axes of the slice: x: 4, y: 4, z: 4, core: 2. Of those that a mesh axis runs over, the one named last changes fastest.
Arguments:
- lower_panel: float32 [1, 4, 512, 8192], P(None, None, 'col', 'row'), may hold values from -4 to 4, as said below
- right_side: float32 [1, 8192, 8192], P(None, 'row', 'col'), may hold values from -6 to 6
Outputs:
- solution: float32 [4, 512, 8192], P(None, None, 'col')
- updated_rhs: float32 [1, 8192, 8192], P(None, 'row', 'col')
Inputs may be any that keep to these rules, and one draw needn't show every extreme that they name: `lower_panel`: L is lower triangular: entries of tiles L[g, s] with g < s and above the diagonal of L[s, s] are zero; the diagonal entries of L lie between 2 and 4.
All inputs are finite; a program needn't handle non-finite values.
Results may differ from a plain program's by a relative error of at most 0.00017.
Values sent between devices are 32-bit elements; how exact they have to be, the bound alone decides.
A program may use at most 128 MiB of HBM per device.

v0:
```python
import jax
import jax.numpy as jnp
from jax import lax
from jax.sharding import Mesh
from jax.sharding import PartitionSpec as P

COL = ("col_0", "col_1")


def joined_along(tiles, dim):
    tiles = jnp.moveaxis(tiles, 0, dim)
    shape = tiles.shape
    return tiles.reshape(*shape[:dim], shape[dim] * shape[dim + 1], *shape[dim + 2 :])


def stacked_from(x, axes, order):
    tiles = x
    for k in order:
        tiles = lax.all_gather(tiles, axes[k])
    done = order[::-1]
    back = [done.index(k) for k in range(len(axes))]
    tiles = tiles.transpose(*back, *range(len(axes), tiles.ndim))
    return tiles.reshape(-1, *x.shape)


def gather_axes(x, axes, order, dim):
    return joined_along(stacked_from(x, axes, order), dim)


def from_root(x, axis, root):
    mine = lax.axis_index(axis) == root
    return lax.psum(jnp.where(mine, x, jnp.zeros_like(x)), axis)


def per_device(lower_panel, right_side):
    rounds = lower_panel.shape[0]
    sections = lower_panel.shape[1]
    block = lower_panel.shape[3]
    my_row = lax.axis_index("row")
    row_count = lax.axis_size("row")
    tile_number = jnp.arange(rounds, dtype=jnp.int32) * row_count + my_row
    current = right_side
    collected = []
    for section in range(sections):
        is_owner = my_row == section
        column = lax.dynamic_index_in_dim(lower_panel, section, 1, keepdims=False)
        diag_tile = gather_axes(column[0], COL, (0, 1), 0).T
        safe_tile = jnp.where(is_owner, diag_tile, jnp.eye(block, dtype=jnp.float32))
        local_solve = lax.linalg.triangular_solve(safe_tile, current[0], left_side=True, lower=True)
        solved = from_root(local_solve, "row", section)
        rows_here = solved
        update = jnp.einsum(
            "rcq,cx->rqx",
            gather_axes(column, COL, (0, 1), 1),
            rows_here,
            precision=lax.Precision.HIGHEST,
        )
        keep_rows = (tile_number > section)[:, None, None]
        current, solved = (current - jnp.where(keep_rows, update, jnp.float32(0.0)), solved)
        collected.append(solved)
    solutions = jnp.stack(collected)
    return (solutions, current)


def solution(mesh):
    torus = Mesh(mesh.devices.reshape(mesh.shape["row"], 4, 2), ("row", "col_0", "col_1"))
    return jax.shard_map(
        per_device,
        mesh=torus,
        in_specs=(P(None, None, COL, "row"), P(None, "row", COL)),
        out_specs=(P(None, None, COL), P(None, "row", COL)),
        check_vma=False,
    )
```

profile of v0, /device:TPU:0, one launch (start us, length us, event | category | flops | bytes accessed | tf_op | source)
XLA Modules:
  0.0 541.8 jit_solution(2427582798928206186)
XLA Ops:
  7.2 1.1 fusion.96
  8.3 14.0 %all-gather = f32[4,1,64,512]{3,2,1,0:T(8,128)} all-gather(f32[1,1,64,512]{3,2,1,0:T(8,128)S(1)} %get-tuple-element.131), channel_id=2, replica_groups=mesh['row'=16,'col_0'=4,'col_1'=2] {'col_0'}, dimensions={0}, use_global_device_ids=true | all-gather | bytes 655360 | tf_op jit(solution)/shard_map/all_gather | solution.py:19
  22.4 13.8 %all-gather.2 = f32[4,1,64,512]{3,2,1,0:T(8,128)} all-gather(f32[1,1,64,512]{3,2,1,0:T(8,128)S(1)} %get-tuple-element.130), channel_id=4, replica_groups=mesh['row'=16,'col_0'=4,'col_1'=2] {'col_0'}, dimensions={0}, use_global_device_ids=true | all-gather | bytes 655360 | tf_op jit(solution)/shard_map/all_gather | solution.py:19
  36.7 1.3 copy.43
  38.8 10.9 %while.8 = (s32[]{:T(128)}, f32[512,512]{0,1:T(8,128)S(1)}, s32[4,2]{0,1:T(2,128)S(1)}, f32[4,128,128]{2,1,0:T(8,128)}, s32[]{:T(128)}) while((s32[]{:T(128)}, f32[512,512]{0,1:T(8,128)S(1)}, s32[4,2]{0,1:T(2,128)S(1)}, f32[4,128,128]{2,1,0:T(8,128)}, s32[]{:T(128)}) %tuple.86), condition=%wide.while_cond, body=%wide.while_body.sunk | while | flops 2 | bytes 393329 | solution.py:49
  39.5 1.3 dynamic-slice.22
  42.2 1.3 dynamic-slice.22
  45.0 1.3 dynamic-slice.22
  47.7 1.3 dynamic-slice.22
  49.8 40.8 %custom-call.6 = f32[4,128,128]{1,2,0:T(8,128)} custom-call(f32[4,128,128]{2,1,0:T(8,128)} %get-tuple-element.29), custom_call_target="InvertDiagBlocksLowerTriangular" | custom-call | tf_op jit(solution)/shard_map/triangular_solve/custom-call.1 | solution.py:49
  90.5 1.5 fusion.58
  94.7 1.1 fusion.33
  96.5 1.6 maximum_select_fusion
  98.1 14.0 %all-gather.5 = f32[4,1,64,512]{3,2,1,0:T(8,128)} all-gather(f32[1,1,64,512]{3,2,1,0:T(8,128)S(1)} %get-tuple-element.132), channel_id=7, replica_groups=mesh['row'=16,'col_0'=4,'col_1'=2] {'col_0'}, dimensions={0}, use_global_device_ids=true | all-gather | bytes 655360 | tf_op jit(solution)/shard_map/all_gather | solution.py:19
  112.2 1.8 copy.48
  114.0 1.1 copy.47
  115.1 1.3 copy.45
  116.6 8.9 %while.9 = (s32[]{:T(128)}, f32[512,512]{0,1:T(8,128)S(1)}, s32[4,2]{0,1:T(2,128)S(1)}, f32[4,128,128]{2,1,0:T(8,128)S(1)}, s32[]{:T(128)}) while((s32[]{:T(128)}, f32[512,512]{0,1:T(8,128)S(1)}, s32[4,2]{0,1:T(2,128)S(1)}, f32[4,128,128]{2,1,0:T(8,128)S(1)}, s32[]{:T(128)}) %tuple.114), condition=%wide.while_cond.clone, body=%wide.while_body.clone.sunk | while | flops 2 | bytes 393329 | solution.py:49
  117.3 1.4 dynamic-slice.24
  119.5 1.4 dynamic-slice.24
  121.7 1.4 dynamic-slice.24
  123.9 1.4 dynamic-slice.24
  125.5 40.2 %custom-call.7 = f32[4,128,128]{1,2,0:T(8,128)} custom-call(f32[4,128,128]{2,1,0:T(8,128)S(1)} %get-tuple-element.30), custom_call_target="InvertDiagBlocksLowerTriangular" | custom-call | tf_op jit(solution)/shard_map/triangular_solve/custom-call.1 | solution.py:49
  165.7 25.9 %all-reduce.5.cloned.1.call-done = f32[512,1024]{1,0:T(8,128)} async-done(((f32[512,1024]{1,0:T(8,128)}), f32[512,1024]{1,0:T(8,128)}) %all-reduce.5.cloned.1.call-update) | async-done | bytes 2097168 | tf_op jit(solution)/shard_map/psum | solution.py:32
  191.5 5.7 %bitcast_subtract_fusion.3 = f32[1,512,1024]{1,2,0:T(8,128)S(1)} fusion(f32[1,512,1024]{1,2,0:T(8,128)} %copy.48, f32[512,1024]{1,0:T(8,128)} %all-reduce.5.cloned.1.call-done, f32[512,512]{1,0:T(8,128)S(1)} %bitcast.209, pred[]{:T(512)S(6)} %gt.16), kind=kOutput, calls=%fused_computation.20 | convolution fusion | flops 3222274048 | bytes 7340033 | tf_op jit(solution)/shard_map/rcq,cx->rqx/dot_general | solution.py:52
  197.9 1.8 convolution_subtract_fusion.6
  200.4 2.8 convolution_subtract_fusion.2
  203.8 3.7 fusion.30
  208.2 1.6 maximum_select_fusion.1
  209.8 14.4 %all-gather.8 = f32[4,1,64,512]{3,2,1,0:T(8,128)} all-gather(f32[1,1,64,512]{3,2,1,0:T(8,128)S(1)} %get-tuple-element.129), channel_id=10, replica_groups=mesh['row'=16,'col_0'=4,'col_1'=2] {'col_0'}, dimensions={0}, use_global_device_ids=true | all-gather | bytes 655360 | tf_op jit(solution)/shard_map/all_gather | solution.py:19
  224.3 1.3 copy.52
  225.7 1.1 fusion.38
  226.8 12.4 %while.10 = (s32[]{:T(128)}, f32[512,512]{0,1:T(8,128)}, s32[4,2]{0,1:T(2,128)S(1)}, f32[4,128,128]{2,1,0:T(8,128)S(1)}, s32[]{:T(128)}) while((s32[]{:T(128)}, f32[512,512]{0,1:T(8,128)}, s32[4,2]{0,1:T(2,128)S(1)}, f32[4,128,128]{2,1,0:T(8,128)S(1)}, s32[]{:T(128)}) %tuple.115), condition=%wide.while_cond.clone.1, body=%wide.while_body.clone.1.sunk | while | flops 2 | bytes 393329 | solution.py:49
  227.5 2.3 dynamic-slice.26
  230.6 2.3 dynamic-slice.26
  233.8 2.3 dynamic-slice.26
  236.9 2.2 dynamic-slice.26
  240.0 50.3 %custom-call.8 = f32[4,128,128]{1,2,0:T(8,128)S(1)} custom-call(f32[4,128,128]{2,1,0:T(8,128)} %copy-done.15), custom_call_target="InvertDiagBlocksLowerTriangular" | custom-call | tf_op jit(solution)/shard_map/triangular_solve/custom-call.1 | solution.py:49
  291.4 9.5 %all-reduce.7.cloned.1.call-done = f32[512,1024]{1,0:T(8,128)} async-done(((f32[512,1024]{1,0:T(8,128)}), f32[512,1024]{1,0:T(8,128)}) %all-reduce.7.cloned.1.call-update) | async-done | bytes 2097168 | tf_op jit(solution)/shard_map/psum | solution.py:32
  300.9 5.4 bitcast_subtract_fusion.2
  306.9 1.9 convolution_subtract_fusion.5
  309.5 2.8 convolution_subtract_fusion.1
  312.9 3.7 fusion.27
  317.3 1.6 maximum_select_fusion.2
  318.9 1.1 copy-done.7
  320.2 1.3 copy.58
  322.6 12.4 %while.11 = (s32[]{:T(128)}, f32[512,512]{0,1:T(8,128)}, s32[4,2]{0,1:T(2,128)S(1)}, f32[4,128,128]{2,1,0:T(8,128)S(1)}, s32[]{:T(128)}) while((s32[]{:T(128)}, f32[512,512]{0,1:T(8,128)}, s32[4,2]{0,1:T(2,128)S(1)}, f32[4,128,128]{2,1,0:T(8,128)S(1)}, s32[]{:T(128)}) %tuple.116), condition=%wide.while_cond.clone.2, body=%wide.while_body.clone.2.sunk | while | flops 2 | bytes 393329 | solution.py:49
  323.3 2.3 dynamic-slice.28
  326.4 2.3 dynamic-slice.28
  329.5 2.3 dynamic-slice.28
  332.6 2.2 dynamic-slice.28
  335.7 40.3 %custom-call.9 = f32[4,128,128]{1,2,0:T(8,128)S(1)} custom-call(f32[4,128,128]{2,1,0:T(8,128)} %copy-done.14), custom_call_target="InvertDiagBlocksLowerTriangular" | custom-call | tf_op jit(solution)/shard_map/triangular_solve/custom-call.1 | solution.py:49
  376.1 34.2 %all-reduce.9.cloned.1.call-done = f32[512,1024]{1,0:T(8,128)} async-done(((f32[512,1024]{1,0:T(8,128)}), f32[512,1024]{1,0:T(8,128)}) %all-reduce.9.cloned.1.call-update) | async-done | bytes 2097168 | tf_op jit(solution)/shard_map/psum | solution.py:32
  410.2 5.1 bitcast_subtract_fusion.1
  416.0 1.9 convolution_subtract_fusion.4
  418.6 2.8 convolution_subtract_fusion
  422.0 3.7 fusion.24
  426.4 1.6 maximum_select_fusion.3
  428.0 1.2 copy-done.8
  429.1 1.1 copy.64
  430.3 88.5 %all-reduce.11.cloned.1.call-done = f32[512,1024]{1,0:T(8,128)} async-done(((f32[512,1024]{1,0:T(8,128)}), f32[512,1024]{1,0:T(8,128)}) %all-reduce.11.cloned.1.call-update) | async-done | bytes 2097168 | tf_op jit(solution)/shard_map/psum | solution.py:32
  518.8 6.9 %bitcast_subtract_fusion = f32[1,512,1024]{1,2,0:T(8,128)} fusion(f32[1,512,1024]{1,2,0:T(8,128)S(1)} %copy-done.3, f32[512,1024]{1,0:T(8,128)} %all-reduce.11.cloned.1.call-done, f32[512,512]{1,0:T(8,128)} %bitcast.211, pred[]{:T(512)S(6)} %gt.19), kind=kOutput, calls=%fused_computation.17 | convolution fusion | flops 3222274048 | bytes 7340033 | tf_op jit(solution)/shard_map/rcq,cx->rqx/dot_general | solution.py:52
  525.8 3.0 copy.65
  528.8 5.8 %pad_maximum_fusion = f32[4,512,1024]{2,1,0:T(8,128)} fusion(f32[1,512,1024]{2,1,0:T(8,128)} %bitcast.199, f32[1,512,1024]{2,1,0:T(8,128)} %bitcast.198, f32[1,512,1024]{2,1,0:T(8,128)} %bitcast.197, f32[1,512,1024]{2,1,0:T(8,128)S(1)} %bitcast.196), kind=kLoop, calls=%fused_computation.8 | loop fusion | flops 6291456 | bytes 16777216 | tf_op jit(solution)/shard_map/stack | solution.py:61
  (142 shorter events, 31.5 us)
Async XLA Ops:
  7.2 29.5 %all-gather.17.cloned.1.call-start = ((), (), s32[]{:S(2)}) async-start(), calls=%async_computation.4 | async-start | bytes 1572864 | tf_op jit(solution)/shard_map/all_gather | solution.py:19
  22.4 92.8 %all-gather.19.cloned.1.call-start = ((), (), s32[]{:S(2)}) async-start(), calls=%async_computation.5 | async-start | bytes 1572864 | tf_op jit(solution)/shard_map/all_gather | solution.py:19
  36.2 155.3 %all-reduce.5.cloned.1.call-start = ((), (), s32[]{:S(2)}) async-start(), calls=%async_computation | async-start | bytes 4194304 | tf_op jit(solution)/shard_map/psum | solution.py:32
  38.0 52.6 %copy-start.4 = (f32[1,512,1024]{2,1,0:T(8,128)S(1)}, f32[1,512,1024]{2,1,0:T(8,128)}, u32[]{:S(2)}) copy-start(f32[1,512,1024]{2,1,0:T(8,128)} %param.5) | copy-start | bytes 6291460
  90.5 2.2 copy-start.13
  98.1 126.2 %all-gather.21.cloned.1.call-start = ((), (), s32[]{:S(2)}) async-start(), calls=%async_computation.6 | async-start | bytes 1572864 | tf_op jit(solution)/shard_map/all_gather | solution.py:19
  112.1 188.8 %all-reduce.7.cloned.1.call-start = ((), (), s32[]{:S(2)}) async-start(), calls=%async_computation.1 | async-start | bytes 4194304 | tf_op jit(solution)/shard_map/psum | solution.py:32
  112.2 1.8 copy-start.9
  116.4 75.1 %copy-start.10 = (f32[4,2,1,64,512]{4,3,1,0,2:T(8,128)S(1)}, f32[4,2,1,64,512]{4,3,1,0,2:T(8,128)}, u32[]{:S(2)}) copy-start(f32[4,2,1,64,512]{4,3,1,0,2:T(8,128)} %copy.47) | copy-start | bytes 3145732
  125.5 66.0 %copy-start.11 = (f32[512,512]{0,1:T(8,128)}, f32[512,512]{0,1:T(8,128)S(1)}, u32[]{:S(2)}) copy-start(f32[512,512]{0,1:T(8,128)S(1)} %get-tuple-element.335) | copy-start | bytes 3145732
  191.5 5.7 %copy-start.12 = (f32[4,128,128]{1,2,0:T(8,128)S(1)}, f32[4,128,128]{1,2,0:T(8,128)}, u32[]{:S(2)}) copy-start(f32[4,128,128]{1,2,0:T(8,128)} %custom-call.7) | copy-start | bytes 786436
  209.8 110.4 %all-gather.23.cloned.1.call-start = ((), (), s32[]{:S(2)}) async-start(), calls=%async_computation.7 | async-start | bytes 1572864 | tf_op jit(solution)/shard_map/all_gather | solution.py:19
  224.3 186.0 %all-reduce.9.cloned.1.call-start = ((), (), s32[]{:S(2)}) async-start(), calls=%async_computation.2 | async-start | bytes 4194304 | tf_op jit(solution)/shard_map/psum | solution.py:32
  225.7 64.6 %copy-start.6 = (f32[8,1,64,512]{3,2,1,0:T(8,128)S(1)}, f32[8,1,64,512]{3,2,1,0:T(8,128)}, u32[]{:S(2)}) copy-start(f32[8,1,64,512]{3,2,1,0:T(8,128)} %all-gather.19.cloned.1.call-done) | copy-start | bytes 3145732
  239.3 0.7 copy-start.15
  306.3 6.6 %copy-start = (f32[1,512,1024]{1,2,0:T(8,128)}, f32[1,512,1024]{1,2,0:T(8,128)S(1)}, u32[]{:S(2)}) copy-start(f32[1,512,1024]{1,2,0:T(8,128)S(1)} %bitcast_subtract_fusion.2) | copy-start | bytes 6291460
  318.8 1.2 copy-start.7
  318.9 199.9 %all-reduce.11.cloned.1.call-start = ((), (), s32[]{:S(2)}) async-start(), calls=%async_computation.3 | async-start | bytes 4194304 | tf_op jit(solution)/shard_map/psum | solution.py:32
  321.5 88.8 %copy-start.1 = (f32[1,512,1024]{1,2,0:T(8,128)S(1)}, f32[1,512,1024]{1,2,0:T(8,128)}, u32[]{:S(2)}) copy-start(f32[1,512,1024]{1,2,0:T(8,128)} %copy-done) | copy-start | bytes 6291460
  335.0 0.7 copy-start.14
  415.4 6.6 %copy-start.2 = (f32[1,512,1024]{1,2,0:T(8,128)}, f32[1,512,1024]{1,2,0:T(8,128)S(1)}, u32[]{:S(2)}) copy-start(f32[1,512,1024]{1,2,0:T(8,128)S(1)} %bitcast_subtract_fusion.1) | copy-start | bytes 6291460
  427.9 1.2 copy-start.8
  427.9 90.9 %copy-start.3 = (f32[1,512,1024]{1,2,0:T(8,128)S(1)}, f32[1,512,1024]{1,2,0:T(8,128)}, u32[]{:S(2)}) copy-start(f32[1,512,1024]{1,2,0:T(8,128)} %copy-done.2) | copy-start | bytes 6291460
  525.7 3.0 copy-start.5
Sparse Core Ops, SparseCore 0:
  22.5 14.1 all-gather.16
  38.3 13.0 all-gather.18
  98.2 93.2 all-reduce.4
  193.0 11.0 all-gather.20
  209.9 90.9 all-reduce.6
  302.4 11.0 all-gather.22
  319.0 91.2 all-reduce.8
  428.1 90.6 all-reduce.10
where the time goes:
time: 551 us; the launch traced here: 542 us
  other arithmetic  186 us (34%)
  waiting for transfers between devices  159 us (29%)
  local copies, waits for them, and re-layouts  63.3 us (11%)
  matrix products  61.9 us (11%)
  blocking collectives  56.1 us (10%)
  between operations  15.1 us (3%)
    another operation x9, other arithmetic, per_device(): lax.linalg.triangular_solve(safe_tile, current[0], left_side=True, lower=...  174 us
    psum x4, waiting for transfers between devices, from_root(): return lax.psum(jnp.where(mine, x, jnp.zeros_like(x)), axis)  158 us
    all_gather x4, blocking collectives, stacked_from(): tiles = lax.all_gather(tiles, axes[k])  56.1 us
    another operation x85, local copies, waits for them, and re-layouts, per_device(): lax.linalg.triangular_solve(safe_tile, current[0], left_side=True, lower=...  44.9 us
    another operation x28, matrix products, per_device(): lax.linalg.triangular_solve(safe_tile, current[0], left_side=True, lower=...  38.7 us
    dot_general x4, matrix products, per_device(): jnp.einsum('rcq,cx->rqx', gather_axes(column, COL, (0, 1), 1), rows_here,...  23.1 us
  transfers between devices with their start and end apart: 8, of which 5 were waited for; matrix products, arithmetic and copies ran while one was open for 50% of the time, Pallas kernels for 0%

commit v1 on v0

v1 whole, which is shorter than its diff:
```python
import functools

import jax
import jax.numpy as jnp
from jax import lax
from jax.experimental import pallas as pl
from jax.experimental.pallas import tpu as pltpu
from jax.sharding import PartitionSpec as P

MESH = pl.DeviceIdType.MESH
NB = 512
CW = 128
A_CHUNKS = (0, 2, 3, 5, 7)
D_CHUNKS = (1, 4, 6)
N_SEND = 260
F32, BF16 = jnp.float32, jnp.bfloat16


def when(cond, fn):
    if cond is None:
        fn()
    else:
        pl.when(cond)(fn)


def gather_kernel(lp, b, g, ll, lo, own_sem, ga, gd, sl, sx, st, ox, ot, send):
    row, col = lax.axis_index("row"), lax.axis_index("col")
    y, z = row // 4, row % 4
    x, core = col // 2, col % 2

    def y_dev(d):
        return ((y + d + 4) % 4 * 4 + z, col)

    def z_dev(d):
        return (y * 4 + (z + d + 4) % 4, col)

    def x_dev(d):
        return (row, (x + d + 4) % 4 * 2 + core)

    partner = (row, x * 2 + 1 - core)
    blocks = [(z + d) % 4 for d in (0, 3, 1, 2)]
    OWN, LEFT, RIGHT, OPP = range(4)
    ops, sends = [], []

    def at(time, fn):
        ops.append((time, len(ops), fn))

    def put(src, dst, sem, dev, cond=None):
        slot = len(sends)

        def make():
            return pltpu.make_async_remote_copy(
                src_ref=src, dst_ref=dst, send_sem=send.at[slot], recv_sem=sem,
                device_id=dev, device_id_type=MESH,
            )

        sends.append((cond, make))
        when(cond, lambda: make().start())

    def got(ref, sem, cond=None):
        def body():
            pltpu.make_async_copy(ref, ref, sem).wait()

        when(cond, body)

    barrier = pltpu.get_barrier_semaphore()
    around = [y_dev(1), y_dev(-1), y_dev(2), z_dev(1), z_dev(-1), x_dev(1), x_dev(-1), partner]
    for dev in around:
        pl.semaphore_signal(barrier, inc=1, device_id=dev, device_id_type=MESH)

    root, other = y == 0, y != 0

    def l_ref(blk, k, j=None):
        return ll.at[blk, blk - k, col if j is None else j]

    def a_ref(blk, c):
        return g.at[blk, :, pl.ds(c * CW, CW)]

    def d_rows(q):
        return pl.ds(pl.multiple_of(q * 128, 128), 128)

    def d_ref(blk, c, q):
        return g.at[blk, d_rows(q), pl.ds(c * CW, CW)]

    for k in range(4):
        when(root & (z >= k), lambda k=k: pltpu.make_async_copy(lp.at[z - k], l_ref(z, k), sl.at[z, k]).start())
    for c in range(8):
        cols = pl.ds(c * CW, CW)
        if c in A_CHUNKS:
            when(root, lambda c=c, cols=cols: pltpu.make_async_copy(b.at[:, cols], a_ref(z, c), ga.at[z, c]).start())
        else:
            when(root, lambda c=c, cols=cols: pltpu.make_async_copy(
                b.at[pl.ds(0, 128), cols], d_ref(z, c, 0), gd.at[z, c, 0]).start())
    own_copies = [pltpu.make_async_copy(lp, lo.at[:, col], own_sem)]
    for cp in own_copies:
        cp.start()

    pl.semaphore_wait(barrier, len(around))

    def x_group(ref_of, xs, ts, cond, parity, t_send, t_fwd, t_last, src=None):
        xl, xr, xo = (x + 3) % 4, (x + 1) % 4, (x + 2) % 4

        def j_of(xx, cc):
            return xx * 2 + cc

        def start():
            s = ref_of(col) if src is None else src
            d = ref_of(col)
            put(s, d, xs.at[x], x_dev(1), cond)
            put(s, d, xs.at[x], x_dev(-1), cond)
            put(s, d, ts.at[x], partner, cond)

        def forward():
            for xx, here in ((xl, parity == 0), (xr, parity == 1)):
                r = ref_of(j_of(xx, core))
                got(r, xs.at[xx], cond)
                if here:
                    put(r, r, xs.at[xx], x_dev(1 if parity == 0 else -1), cond)
                put(r, r, ts.at[xx], partner, cond)

        def last():
            r = ref_of(j_of(xo, core))
            got(r, xs.at[xo], cond)
            put(r, r, ts.at[xo], partner, cond)

        def done():
            for xx in range(4):
                r = ref_of(j_of(xx, 1 - core))
                got(r, ts.at[xx], cond)

        at(t_send, start)
        at(t_fwd, forward)
        at(t_last, last)
        at(1000.0, done)

    for k in range(4):
        conds = [None if k == 0 else blk >= k for blk in blocks]

        def l_stage0(k=k, conds=conds):
            blk, cond = blocks[OWN], conds[OWN]
            r = l_ref(blk, k)
            got(r, sl.at[blk, k], cond)
            plus = k % 2 == 0
            go = (y != 3) if plus else (y != 1)
            put(r, r, sl.at[blk, k], y_dev(1 if plus else -1), go if cond is None else go & cond)
            put(r, r, sl.at[blk, k], z_dev(1), cond)
            put(r, r, sl.at[blk, k], z_dev(-1), cond)

        def l_stage1(k=k, conds=conds):
            for w in (LEFT, RIGHT):
                blk, cond = blocks[w], conds[w]
                r = l_ref(blk, k)
                got(r, sl.at[blk, k], cond)
                if (k % 2 == 0) == (w == LEFT):
                    put(r, r, sl.at[blk, k], z_dev(1 if w == LEFT else -1), cond)

        def l_stage2(k=k, conds=conds):
            blk, cond = blocks[OPP], conds[OPP]
            got(l_ref(blk, k), sl.at[blk, k], cond)

        at(2.0 + 2 * k, l_stage0)
        at(5.0 + 2 * k, l_stage1)
        at(8.0 + 2 * k, l_stage2)
        ready = (2.1 + 2 * k, 5.1 + 2 * k, 5.2 + 2 * k, 8.1 + 2 * k)
        for w in range(4):
            i = 4 * k + w
            x_group(
                lambda j, blk=blocks[w], k=k: l_ref(blk, k, j), sx.at[blocks[w], k], st.at[blocks[w], k],
                conds[w], i % 2, ready[w], 9.0 + 2.7 * i, 14.0 + 2.7 * i,
            )
    for h in range(2):
        def o_ref(j, h=h):
            return lo.at[pl.ds(2 * h, 2), j]

        x_group(o_ref, ox.at[h], ot.at[h], None, h, 12.0 + h, 46.0 + 3 * h, 52.0 + 3 * h,
                src=lp.at[pl.ds(2 * h, 2)])

    order = (0, 1, 2, 3, 4, 5, 6, 7)
    for i, c in enumerate(order):
        t = 5.0 + 6.0 * i
        if c in A_CHUNKS:
            n = A_CHUNKS.index(c)

            def a_stage0(c=c, n=n):
                r = a_ref(z, c)
                got(r, ga.at[z, c])
                plus = n % 2 == 0
                put(r, r, ga.at[z, c], y_dev(1 if plus else -1), (y != 3) if plus else (y != 1))
                put(r, r, ga.at[z, c], z_dev(1))
                put(r, r, ga.at[z, c], z_dev(-1))

            def a_stage1(c=c, n=n):
                for w in (LEFT, RIGHT):
                    blk = blocks[w]
                    r = a_ref(blk, c)
                    got(r, ga.at[blk, c])
                    if (n % 2 == 0) == (w == LEFT):
                        put(r, r, ga.at[blk, c], z_dev(1 if w == LEFT else -1))

            def a_stage2(c=c):
                blk = blocks[OPP]
                got(a_ref(blk, c), ga.at[blk, c])

            at(t, a_stage0)
            at(t + 7, a_stage1)
            at(t + 100, a_stage2)
        else:
            n = D_CHUNKS.index(c)

            def d_scatter(c=c):
                for q in (1, 3, 2):
                    put(b.at[pl.ds(q * 128, 128), pl.ds(c * CW, CW)], d_ref(z, c, q), gd.at[z, c, q], y_dev(q), root)

            def d_y(w, c=c):
                blk = blocks[w]
                r = d_ref(blk, c, y)
                put(r, r, gd.at[blk, c, y], y_dev(1))
                put(r, r, gd.at[blk, c, y], y_dev(-1))

            def d_stage0(c=c, d_y=d_y):
                r = d_ref(z, c, y)
                got(r, gd.at[z, c, y])
                put(r, r, gd.at[z, c, y], z_dev(1))
                put(r, r, gd.at[z, c, y], z_dev(-1))
                d_y(OWN)

            def d_stage1(c=c, n=n, d_y=d_y):
                for w in (LEFT, RIGHT):
                    blk = blocks[w]
                    r = d_ref(blk, c, y)
                    got(r, gd.at[blk, c, y])
                    if (n % 2 == 0) == (w == LEFT):
                        put(r, r, gd.at[blk, c, y], z_dev(1 if w == LEFT else -1))
                    d_y(w)

            def d_stage2(c=c, d_y=d_y):
                blk = blocks[OPP]
                got(d_ref(blk, c, y), gd.at[blk, c, y])
                d_y(OPP)

            def d_fwd(w, c=c):
                blk = blocks[w]
                for d in (-1, 1):
                    q = (y + d + 4) % 4
                    r = d_ref(blk, c, q)
                    got(r, gd.at[blk, c, q])
                    if (w % 2 == 0) == (d == -1):
                        put(r, r, gd.at[blk, c, q], y_dev(-d))

            def d_end(c=c):
                for blk in blocks:
                    q = (y + 2) % 4
                    got(d_ref(blk, c, q), gd.at[blk, c, q])

            at(1.0 + 0.1 * i if i < 2 else t - 8, d_scatter)
            at(t, d_stage0)
            at(t + 4, d_stage1)
            at(t + 7, d_stage2)
            at(t + 5, functools.partial(d_fwd, OWN))
            at(t + 9, functools.partial(d_fwd, LEFT))
            at(t + 9.1, functools.partial(d_fwd, RIGHT))
            at(t + 12, functools.partial(d_fwd, OPP))
            at(t + 100, d_end)

    for _, _, fn in sorted(ops, key=lambda o: o[:2]):
        fn()
    for cond, make in sends:
        when(cond, lambda make=make: make().wait_send())
    for cp in own_copies:
        cp.wait()


def dot(a, b):
    return jnp.dot(a, b, preferred_element_type=F32)


def exact(a, b):
    return jnp.dot(a, b, preferred_element_type=F32, precision=lax.Precision.HIGHEST)


def split(v):
    hi = v.astype(BF16)
    return hi, (v - hi.astype(F32)).astype(BF16)


def invert_tiles(tiles):
    n = 128
    ri = lax.broadcasted_iota(jnp.int32, (n, n), 0)
    ci = lax.broadcasted_iota(jnp.int32, (n, n), 1)
    eye = ri == ci
    ident = jnp.where(eye, F32(1.0), F32(0.0))
    count = len(tiles)
    scaled, inv_row, parts = [], [], []
    for t in tiles:
        cols, rows = [], []
        for d in range(4):
            blk = t[d * n:(d + 1) * n, d * n:(d + 1) * n]
            diag = jnp.where(eye, blk, F32(0.0))
            cols.append(F32(1.0) / jnp.sum(diag, axis=1, keepdims=True))
            rows.append(F32(1.0) / jnp.sum(diag, axis=0, keepdims=True))
        scaled.append(t * jnp.concatenate(cols, axis=0))
        inv_row.append(jnp.concatenate(rows, axis=1))
    for t in scaled:
        for d in range(4):
            parts.append(jnp.where(ri > ci, t[d * n:(d + 1) * n, d * n:(d + 1) * n], F32(0.0)))
    same8 = (ri // 8) == (ci // 8)
    small = [jnp.where(same8, p, F32(0.0)) for p in parts]
    sq = [exact(m, m) for m in small]
    inv = [(ident - m) for m in small]
    step = [exact(v, q) for v, q in zip(inv, sq)]
    quad = [exact(q, q) for q in sq]
    inv = [v + s for v, s in zip(inv, step)]
    step = [exact(v, q) for v, q in zip(inv, quad)]
    inv = [v + s for v, s in zip(inv, step)]
    for w in (8, 16, 32, 64):
        mask = (ri // (2 * w) == ci // (2 * w)) & ((ri // w) != (ci // w))
        low = [exact(jnp.where(mask, p, F32(0.0)), v) for p, v in zip(parts, inv)]
        step = [exact(v, s) for v, s in zip(inv, low)]
        inv = [v - s for v, s in zip(inv, step)]
    zero = jnp.zeros((n, n), F32)
    pairs = []
    low = []
    for k in range(count):
        for h in range(2):
            a, c = 2 * h, 2 * h + 1
            low.append(exact(scaled[k][c * n:(c + 1) * n, a * n:(a + 1) * n], inv[4 * k + a]))
    for k in range(count):
        for h in range(2):
            a, c = inv[4 * k + 2 * h], inv[4 * k + 2 * h + 1]
            e = -exact(c, low[2 * k + h])
            pairs.append(jnp.concatenate(
                [jnp.concatenate([a, zero], axis=1), jnp.concatenate([e, c], axis=1)], axis=0))
    low = [exact(scaled[k][256:, :256], pairs[2 * k]) for k in range(count)]
    zero = jnp.zeros((256, 256), F32)
    out = []
    for k in range(count):
        e = -exact(pairs[2 * k + 1], low[k])
        full = jnp.concatenate(
            [jnp.concatenate([pairs[2 * k], zero], axis=1), jnp.concatenate([e, pairs[2 * k + 1]], axis=1)], axis=0)
        out.append(full * inv_row[k])
    return out


def solve_kernel(g, ll, lo, b, x_out, c_out, lh, lw, vh, vw, oh, ow, xh, xw):
    row = lax.axis_index("row")

    @pl.when(pl.program_id(0) == 0)
    def _():
        for r in range(4):
            for s in range(r):
                cols = pl.ds(s * NB, NB)
                lh[r - 1, :, cols], lw[r - 1, :, cols] = split(ll[r, s].T)
        for s in range(4):
            cols = pl.ds(s * NB, NB)
            oh[:, cols], ow[:, cols] = split(jnp.where(row > s, lo[s], F32(0.0)).T)
        for s, v in enumerate(invert_tiles([ll[s, s].T for s in range(4)])):
            vh[s], vw[s] = split(v)

    for r in range(4):
        rhs = g[r]
        if r:
            k = pl.ds(0, r * NB)
            a, aw, v, vv = lh[r - 1, :, k], lw[r - 1, :, k], xh[k, :], xw[k, :]
            rhs = rhs - (dot(a, v) + (dot(a, vv) + dot(aw, v)))
        hi, low = split(rhs)
        out = dot(vh[r], hi) + (dot(vh[r], low) + dot(vw[r], hi))
        x_out[r] = out
        rows = pl.ds(r * NB, NB)
        xh[rows, :], xw[rows, :] = split(out)
    upd = dot(oh[...], xh[...]) + (dot(oh[...], xw[...]) + dot(ow[...], xh[...]))
    c_out[...] = b[...] - upd


def per_device(lower_panel, right_side):
    lp, b = lower_panel[0], right_side[0]
    width = b.shape[1]
    dma = pltpu.SemaphoreType.DMA
    hbm = pl.BlockSpec(memory_space=pl.ANY)
    g, ll, lo = pl.pallas_call(
        gather_kernel,
        out_shape=(
            jax.ShapeDtypeStruct((4, NB, width), F32),
            jax.ShapeDtypeStruct((4, 4, 8, 64, NB), F32),
            jax.ShapeDtypeStruct((4, 8, 64, NB), F32),
        ),
        in_specs=[hbm, hbm],
        out_specs=(hbm, hbm, hbm),
        scratch_shapes=[
            dma(()), dma((4, 8)), dma((4, 8, 4)), dma((4, 4)), dma((4, 4, 4)), dma((4, 4, 4)),
            dma((2, 4)), dma((2, 4)), dma((N_SEND,)),
        ],
        compiler_params=pltpu.CompilerParams(collective_id=0, has_side_effects=True),
        name="gather",
    )(lp, b)
    ll = ll.reshape(4, 4, NB, NB)
    lo = lo.reshape(4, NB, NB)
    w = 256
    vmem = pl.BlockSpec(memory_space=pltpu.VMEM)
    x, c = pl.pallas_call(
        solve_kernel,
        grid=(width // w,),
        out_shape=(jax.ShapeDtypeStruct((4, NB, width), F32), jax.ShapeDtypeStruct((NB, width), F32)),
        in_specs=[
            pl.BlockSpec((4, NB, w), lambda i: (0, 0, i)), vmem, vmem,
            pl.BlockSpec((NB, w), lambda i: (0, i)),
        ],
        out_specs=(pl.BlockSpec((4, NB, w), lambda i: (0, 0, i)), pl.BlockSpec((NB, w), lambda i: (0, i))),
        scratch_shapes=[
            pltpu.VMEM((3, NB, 3 * NB), BF16), pltpu.VMEM((3, NB, 3 * NB), BF16),
            pltpu.VMEM((4, NB, NB), BF16), pltpu.VMEM((4, NB, NB), BF16),
            pltpu.VMEM((NB, 4 * NB), BF16), pltpu.VMEM((NB, 4 * NB), BF16),
            pltpu.VMEM((4 * NB, w), BF16), pltpu.VMEM((4 * NB, w), BF16),
        ],
        compiler_params=pltpu.CompilerParams(vmem_limit_bytes=66_000_000),
        name="solve",
    )(g, ll, lo, b)
    return x, c[None]


def solution(mesh):
    return jax.shard_map(
        per_device,
        mesh=mesh,
        in_specs=(P(None, None, "col", "row"), P(None, "row", "col")),
        out_specs=(P(None, None, "col"), P(None, "row", "col")),
        check_vma=False,
    )
```

time: 551 us -> 248 us (0.45); the launches traced: 542 us -> 247 us
  Pallas kernels: 0 us -> 246 us
  other arithmetic: 186 us -> 0 us
  waiting for transfers between devices: 159 us -> 0 us
  local copies, waits for them, and re-layouts: 63.3 us -> 0 us
  matrix products: 61.9 us -> 0 us
  blocking collectives: 56.1 us -> 0 us
  between operations: 15.1 us -> 0.64 us
    pallas_call x0 -> x2, Pallas kernels: none -> 246 us  [the longest x1 175 us: per_device(): pl.pallas_call(gather_kernel, out_shape=(jax.ShapeDtypeStruct((4, NB, wid...]
    another operation x10 -> x0, other arithmetic: 180 us -> none  [the longest x9 174 us: per_device(): lax.linalg.triangular_solve(safe_tile, current[0], left_side=True, lower=...]
    psum x4 -> x0, waiting for transfers between devices: 158 us -> none  [from_root(): return lax.psum(jnp.where(mine, x, jnp.zeros_like(x)), axis)]
    all_gather x4 -> x0, blocking collectives: 56.1 us -> none  [stacked_from(): tiles = lax.all_gather(tiles, axes[k])]
    another operation x85 -> x0, local copies, waits for them, and re-layouts: 44.9 us -> none  [per_device(): lax.linalg.triangular_solve(safe_tile, current[0], left_side=True, lower=...]
    another operation x28 -> x0, matrix products: 38.7 us -> none  [per_device(): lax.linalg.triangular_solve(safe_tile, current[0], left_side=True, lower=...]
    dot_general x4 -> x0, matrix products: 23.1 us -> none  [per_device(): jnp.einsum('rcq,cx->rqx', gather_axes(column, COL, (0, 1), 1), rows_here,...]
    unnamed x34 -> x0, local copies, waits for them, and re-layouts: 8.63 us -> none
  transfers between devices with their start and end apart: 8 -> 0, of which waited for: 5 -> 0; matrix products, arithmetic and copies ran while one was open for 50% -> 0% of each run, Pallas kernels for 0% -> 0%
where the time goes in v1:
time: 248 us; the launch traced here: 247 us
  Pallas kernels  246 us (99%)
    pallas_call x1, Pallas kernels, per_device(): pl.pallas_call(gather_kernel, out_shape=(jax.ShapeDtypeStruct((4, NB, wid...  175 us
    pallas_call x1, Pallas kernels, per_device(): pl.pallas_call(solve_kernel, grid=(width // w,), out_shape=(jax.ShapeDtyp...  71.1 us

profile of v1, /device:TPU:0, one launch (start us, length us, event | category | flops | bytes accessed | tf_op | source)
XLA Modules:
  0.0 246.9 jit_solution(709929800634385046)
XLA Ops:
  0.6 175.2 %gather.1 = (f32[4,512,1024]{2,1,0:T(8,128)}, f32[4,4,8,64,512]{4,3,2,1,0:T(8,128)}, f32[4,8,64,512]{3,2,1,0:T(8,128)}) custom-call(f32[4,64,512]{2,1,0:T(8,128)} %bitcast.9, f32[512,1024]{1,0:T(8,128)} %bitcast.6), custom_call_target="tpu_custom_call" | custom-call | tf_op jit(solution)/shard_map/gather/pallas_call | solution.py:379
  175.8 71.1 %solve.1 = (f32[4,512,1024]{2,1,0:T(8,128)}, f32[512,1024]{1,0:T(8,128)}) custom-call(f32[4,512,1024]{2,1,0:T(8,128)} %get-tuple-element.7.g, f32[4,4,512,512]{3,2,1,0:T(8,128)} %bitcast.5, f32[4,512,512]{2,1,0:T(8,128)} %bitcast.8, f32[512,1024]{1,0:T(8,128)} %bitcast.7), custom_call_target="tpu_custom_call" | custom-call | tf_op jit(solution)/shard_map/solve/pallas_call | solution.py:399

commit v2 on v1

v2 whole, which is shorter than its diff:
```python
import functools

import jax
import jax.numpy as jnp
from jax import lax
from jax.experimental import pallas as pl
from jax.experimental.pallas import tpu as pltpu
from jax.sharding import PartitionSpec as P

MESH = pl.DeviceIdType.MESH
NB = 512
CW = 128
Z_FIRST = (2, 5, 7)
N_SEND = 400
TIMES = (11, 17, 25, 29, 30, 38, 48, 75, 66, 83, 141, 190, 104, 157, 87, 119, 169, 112, 100, 185, 0, 1, 12, 7, 13, 28, 23, 36, 156, 130, 164, 40, 126, 93, 99, 43, 68, 61, 178, 122, 31, 39, 41, 51, 52, 74, 73, 84, 110, 64, 193, 123, 135, 161, 90, 133, 196, 121, 114, 150, 2, 3, 21, 8, 22, 49, 44, 71, 129, 80, 175, 142, 116, 170, 95, 155, 172, 105, 163, 138, 6, 32, 20, 62, 14, 117, 58, 146, 10, 109, 176, 139, 27, 82, 65, 97, 4, 9, 16, 19, 35, 63, 162, 188, 120, 45, 103, 127, 106, 5, 15, 47, 24, 76, 101, 181, 145, 115, 195, 60, 91, 191, 26, 34, 56, 50, 69, 140, 166, 152, 186, 57, 183, 111, 107, 18, 33, 37, 59, 128, 86, 85, 165, 154, 102, 77, 158, 174, 46, 55, 78, 89, 98, 113, 173, 182, 147, 180, 177, 192, 143, 42, 53, 70, 94, 124, 134, 72, 118, 149, 194, 144, 168, 131, 67, 81, 92, 96, 137, 151, 167, 179, 171, 197, 159, 198, 199, 54, 79, 108, 88, 125, 160, 148, 136, 132, 153, 187, 184, 189)
F32, BF16 = jnp.float32, jnp.bfloat16


def when(cond, fn):
    if cond is None:
        fn()
    else:
        pl.when(cond)(fn)


def gather_kernel(lp, b, g, ll, lo, own_sem, gs, sq, sl, sx, st, ox, ot, send):
    row, col = lax.axis_index("row"), lax.axis_index("col")
    y, z = row // 4, row % 4
    x, core = col // 2, col % 2

    def y_dev(d):
        return ((y + d + 4) % 4 * 4 + z, col)

    def z_dev(d):
        return (y * 4 + (z + d + 4) % 4, col)

    def x_dev(d):
        return (row, (x + d + 4) % 4 * 2 + core)

    partner = (row, x * 2 + 1 - core)
    blocks = [(z + d) % 4 for d in (0, 3, 1, 2)]
    OWN, LEFT, RIGHT, OPP = range(4)
    ops, ends, sends = [], [], []
    task, last = ops.append, ends.append

    def put(src, dst, sem, dev, cond=None):
        slot = len(sends)

        def make():
            return pltpu.make_async_remote_copy(
                src_ref=src, dst_ref=dst, send_sem=send.at[slot], recv_sem=sem,
                device_id=dev, device_id_type=MESH,
            )

        sends.append((cond, make))
        when(cond, lambda: make().start())

    def got(ref, sem, cond=None):
        def body():
            pltpu.make_async_copy(ref, ref, sem).wait()

        when(cond, body)

    barrier = pltpu.get_barrier_semaphore()
    around = [y_dev(1), y_dev(-1), y_dev(2), z_dev(1), z_dev(-1), x_dev(1), x_dev(-1), partner]
    for dev in around:
        pl.semaphore_signal(barrier, inc=1, device_id=dev, device_id_type=MESH)

    root, other = y == 0, y != 0

    def l_ref(blk, k, j=None):
        return ll.at[blk, blk - k, col if j is None else j]

    def piece(blk, c, q):
        return g.at[blk, pl.ds(pl.multiple_of(q * 128, 128), 128), pl.ds(c * CW, CW)]

    def l_quarter(k, q):
        return ll.at[z, z - k, col, pl.ds(pl.multiple_of(q * 16, 16), 16)]

    for k in range(4):
        when(root & (z >= k), lambda k=k: pltpu.make_async_copy(
            lp.at[z - k, pl.ds(0, 16)], l_quarter(k, 0), sq.at[k, 0]).start())
    for c in range(8):
        when(root, lambda c=c: pltpu.make_async_copy(
            b.at[pl.ds(0, 128), pl.ds(c * CW, CW)], piece(z, c, 0), gs.at[z, c, 0]).start())
    own_copies = [pltpu.make_async_copy(lp, lo.at[:, col], own_sem)]
    for cp in own_copies:
        cp.start()

    pl.semaphore_wait(barrier, len(around))

    def x_group(ref_of, xs, ts, cond, parity, src=None):
        def j_of(xx, cc):
            return xx * 2 + cc

        def start():
            s = ref_of(col) if src is None else src
            d = ref_of(col)
            put(s, d, xs.at[x], x_dev(1), cond)
            put(s, d, xs.at[x], x_dev(-1), cond)
            put(s, d, ts.at[x], partner, cond)

        def arrive(d, relay):
            xx = (x + d + 4) % 4
            r = ref_of(j_of(xx, core))
            got(r, xs.at[xx], cond)
            if relay:
                put(r, r, xs.at[xx], x_dev(-d), cond)
            put(r, r, ts.at[xx], partner, cond)

        def done():
            for xx in range(4):
                got(ref_of(j_of(xx, 1 - core)), ts.at[xx], cond)

        return start, arrive, done

    for k in range(4):
        conds = [None if k == 0 else blk >= k for blk in blocks]
        groups = [
            x_group(lambda j, blk=blocks[w], k=k: l_ref(blk, k, j), sx.at[blocks[w], k], st.at[blocks[w], k],
                    conds[w], (k + w) % 2)
            for w in range(4)
        ]

        def l_scatter(k=k, cond=conds[OWN]):
            for q in (1, 3, 2):
                put(lp.at[z - k, pl.ds(q * 16, 16)], l_quarter(k, q), sq.at[k, q], y_dev(q),
                    root if cond is None else root & cond)

        def l_mine(k=k, cond=conds[OWN]):
            r, sem = l_quarter(k, y), sq.at[k, y]
            got(r, sem, cond)
            put(r, r, sem, y_dev(1), cond)
            put(r, r, sem, y_dev(-1), cond)

        def l_relay(d, k=k, cond=conds[OWN]):
            q = (y + d + 4) % 4
            r, sem = l_quarter(k, q), sq.at[k, q]
            got(r, sem, cond)
            if d == (-1 if k % 2 == 0 else 1):
                put(r, r, sem, y_dev(-d), cond)

        def l_own(k=k, cond=conds[OWN], start=groups[OWN][0]):
            q = (y + 2) % 4
            got(l_quarter(k, q), sq.at[k, q], cond)
            r, sem = l_ref(z, k), sl.at[z, k]
            put(r, r, sem, z_dev(1), cond)
            put(r, r, sem, z_dev(-1), cond)
            start()

        def l_arrive(w, k=k, conds=conds, groups=groups):
            blk, cond = blocks[w], conds[w]
            r, sem = l_ref(blk, k), sl.at[blk, k]
            got(r, sem, cond)
            if w == (LEFT if k % 2 == 0 else RIGHT):
                put(r, r, sem, z_dev(1 if w == LEFT else -1), cond)
            groups[w][0]()

        task(l_scatter)
        task(l_mine)
        task(functools.partial(l_relay, -1))
        task(functools.partial(l_relay, 1))
        task(l_own)
        for w in (LEFT, RIGHT, OPP):
            task(functools.partial(l_arrive, w))
        for w in range(4):
            for d in (-1, 1, 2):
                task(functools.partial(groups[w][1], d, d == (-1 if (k + w) % 2 == 0 else 1)))
            last(groups[w][2])
    for h in range(4):
        start, arrive, done = x_group(lambda j, h=h: lo.at[h, j], ox.at[h], ot.at[h], None, h % 2, src=lp.at[h])
        task(start)
        for d in (-1, 1, 2):
            task(functools.partial(arrive, d, d == (-1 if h % 2 == 0 else 1)))
        last(done)

    for c in range(8):
        def scatter(c=c):
            for q in (1, 3, 2):
                put(b.at[pl.ds(q * 128, 128), pl.ds(c * CW, CW)], piece(z, c, q), gs.at[z, c, q], y_dev(q), root)

        zfirst = c in Z_FIRST
        pos1, pos2 = (z, y) if zfirst else (y, z)
        dev1, dev2 = (z_dev, y_dev) if zfirst else (y_dev, z_dev)

        def at(e, d, c=c, pos1=pos1, pos2=pos2, zfirst=zfirst):
            i1, i2 = (pos1 + e + 4) % 4, (pos2 + d + 4) % 4
            blk, q = (i1, i2) if zfirst else (i2, i1)
            return piece(blk, c, q), gs.at[blk, c, q]

        def first(e, c=c, at=at, dev1=dev1, dev2=dev2):
            r, sem = at(e, 0)
            got(r, sem)
            if e == 0:
                put(r, r, sem, dev1(1))
                put(r, r, sem, dev1(-1))
            elif e == (-1 if c // 2 % 2 == 0 else 1):
                put(r, r, sem, dev1(-e))
            put(r, r, sem, dev2(1))
            put(r, r, sem, dev2(-1))

        def second(e, d, at=at, dev2=dev2):
            r, sem = at(e, d)
            got(r, sem)
            if d == (-1 if e in (0, 2) else 1):
                put(r, r, sem, dev2(-d))

        task(scatter)
        for e in (0, -1, 1, 2):
            task(functools.partial(first, e))
        for e in (0, -1, 1, 2):
            for d in (-1, 1):
                task(functools.partial(second, e, d))
            last(functools.partial(second, e, 2))

    order = sorted(range(len(ops)), key=lambda i: (TIMES[i] if i < len(TIMES) else i, i))
    for i in order:
        ops[i]()
    for fn in ends:
        fn()
    for cond, make in sends:
        when(cond, lambda make=make: make().wait_send())
    for cp in own_copies:
        cp.wait()


def dot(a, b):
    return jnp.dot(a, b, preferred_element_type=F32)


def split(v):
    hi = v.astype(BF16)
    return hi, (v - hi.astype(F32)).astype(BF16)


def dot_small(a, b):
    bb = jnp.concatenate(split(b), axis=1)
    r = dot(jnp.concatenate(split(a), axis=1), jnp.concatenate([bb, bb], axis=0))
    return r[:, :128] + r[:, 128:]


def dot3(a, b):
    (ah, al), (bh, bl) = split(a), split(b)
    return dot(ah, bh) + (dot(ah, bl) + dot(al, bh))


def invert_tiles(tiles):
    n = 128
    ri = lax.broadcasted_iota(jnp.int32, (n, n), 0)
    ci = lax.broadcasted_iota(jnp.int32, (n, n), 1)
    eye = ri == ci
    ident = jnp.where(eye, F32(1.0), F32(0.0))
    count = len(tiles)
    scaled, inv_row, parts = [], [], []
    for t in tiles:
        cols, rows = [], []
        for d in range(4):
            blk = t[d * n:(d + 1) * n, d * n:(d + 1) * n]
            diag = jnp.where(eye, blk, F32(0.0))
            cols.append(F32(1.0) / jnp.sum(diag, axis=1, keepdims=True))
            rows.append(F32(1.0) / jnp.sum(diag, axis=0, keepdims=True))
        scaled.append([[t[a * n:(a + 1) * n, c * n:(c + 1) * n] * cols[a] for c in range(a + 1)] for a in range(4)])
        inv_row.append(jnp.concatenate(rows, axis=1))
    for t in scaled:
        for d in range(4):
            parts.append(jnp.where(ri > ci, t[d][d], F32(0.0)))
    same8 = (ri // 8) == (ci // 8)
    small = [jnp.where(same8, p, F32(0.0)) for p in parts]
    sq = [dot_small(m, m) for m in small]
    inv = [(ident - m) for m in small]
    step = [dot_small(v, q) for v, q in zip(inv, sq)]
    quad = [dot_small(q, q) for q in sq]
    inv = [v + s for v, s in zip(inv, step)]
    step = [dot_small(v, q) for v, q in zip(inv, quad)]
    inv = [v + s for v, s in zip(inv, step)]
    for w in (8, 16, 32, 64):
        mask = (ri // (2 * w) == ci // (2 * w)) & ((ri // w) != (ci // w))
        low = [dot_small(jnp.where(mask, p, F32(0.0)), v) for p, v in zip(parts, inv)]
        step = [dot_small(v, s) for v, s in zip(inv, low)]
        inv = [v - s for v, s in zip(inv, step)]
    zero = jnp.zeros((n, n), F32)
    pairs, low = [], []
    for k in range(count):
        for h in range(2):
            low.append(dot_small(scaled[k][2 * h + 1][2 * h], inv[4 * k + 2 * h]))
    for k in range(count):
        for h in range(2):
            a, c = inv[4 * k + 2 * h], inv[4 * k + 2 * h + 1]
            e = -dot_small(c, low[2 * k + h])
            pairs.append(jnp.concatenate(
                [jnp.concatenate([a, zero], axis=1), jnp.concatenate([e, c], axis=1)], axis=0))
    low = []
    for k in range(count):
        t = scaled[k]
        corner = jnp.concatenate(
            [jnp.concatenate(t[2][:2], axis=1), jnp.concatenate(t[3][:2], axis=1)], axis=0)
        low.append(dot3(corner, pairs[2 * k]))
    zero = jnp.zeros((256, 256), F32)
    out = []
    for k in range(count):
        e = -dot3(pairs[2 * k + 1], low[k])
        full = jnp.concatenate(
            [jnp.concatenate([pairs[2 * k], zero], axis=1), jnp.concatenate([e, pairs[2 * k + 1]], axis=1)], axis=0)
        out.append(full * inv_row[k])
    return out


STACK = (0, 2048, 3584, 4608, 5120)


def solve_kernel(g, ll, lo, b, x_out, c_out, tiles, sh, sw, vh, vw, acc, sems):
    row = lax.axis_index("row")

    @pl.when(pl.program_id(0) == 0)
    def _():
        wanted = [("d", s, s) for s in range(4)]
        wanted += [("l", r, s) for s in range(4) for r in range(s + 1, 4)]
        wanted += [("o", 0, s) for s in range(4)]
        copies = [
            pltpu.make_async_copy(lo.at[s] if kind == "o" else ll.at[r, s], tiles.at[n], sems.at[n])
            for n, (kind, r, s) in enumerate(wanted)
        ]
        for cp in copies:
            cp.start()
        for cp in copies[:4]:
            cp.wait()
        for s, v in enumerate(invert_tiles([tiles[s].T for s in range(4)])):
            vh[s], vw[s] = split(v)
        for n, (kind, r, s) in enumerate(wanted):
            if n < 4:
                continue
            copies[n].wait()
            t = tiles[n]
            if kind == "o":
                t = jnp.where(row > s, t, F32(0.0))
                rows = pl.ds(STACK[s + 1] - NB, NB)
            else:
                rows = pl.ds(STACK[s] + (r - s - 1) * NB, NB)
            sh[rows, :], sw[rows, :] = split(t.T)

    for s in range(4):
        hi, low = split(g[0] if s == 0 else acc[s - 1])
        x = dot(vh[s], hi) + (dot(vh[s], low) + dot(vw[s], hi))
        x_out[s] = x
        hi, low = split(x)
        rows = pl.ds(STACK[s], STACK[s + 1] - STACK[s])
        upd = dot(sh[rows, :], hi) + (dot(sh[rows, :], low) + dot(sw[rows, :], hi))
        for r in range(s + 1, 4):
            base = g[r] if s == 0 else acc[r - 1]
            acc[r - 1] = base - upd[(r - s - 1) * NB:(r - s) * NB]
        own = (b[...] if s == 0 else acc[3]) - upd[(3 - s) * NB:]
        if s == 3:
            c_out[...] = own
        else:
            acc[3] = own


def per_device(lower_panel, right_side):
    lp, b = lower_panel[0], right_side[0]
    width = b.shape[1]
    dma = pltpu.SemaphoreType.DMA
    hbm = pl.BlockSpec(memory_space=pl.ANY)
    g, ll, lo = pl.pallas_call(
        gather_kernel,
        out_shape=(
            jax.ShapeDtypeStruct((4, NB, width), F32),
            jax.ShapeDtypeStruct((4, 4, 8, 64, NB), F32),
            jax.ShapeDtypeStruct((4, 8, 64, NB), F32),
        ),
        in_specs=[hbm, hbm],
        out_specs=(hbm, hbm, hbm),
        scratch_shapes=[
            dma(()), dma((4, 8, 4)), dma((4, 4)), dma((4, 4)), dma((4, 4, 4)), dma((4, 4, 4)),
            dma((4, 4)), dma((4, 4)), dma((N_SEND,)),
        ],
        compiler_params=pltpu.CompilerParams(collective_id=0, has_side_effects=True),
        name="gather",
    )(lp, b)
    ll = ll.reshape(4, 4, NB, NB)
    lo = lo.reshape(4, NB, NB)
    w = 512
    x, c = pl.pallas_call(
        solve_kernel,
        grid=(width // w,),
        out_shape=(jax.ShapeDtypeStruct((4, NB, width), F32), jax.ShapeDtypeStruct((NB, width), F32)),
        in_specs=[
            pl.BlockSpec((4, NB, w), lambda i: (0, 0, i)), hbm, hbm,
            pl.BlockSpec((NB, w), lambda i: (0, i)),
        ],
        out_specs=(pl.BlockSpec((4, NB, w), lambda i: (0, 0, i)), pl.BlockSpec((NB, w), lambda i: (0, i))),
        scratch_shapes=[
            pltpu.VMEM((14, NB, NB), F32),
            pltpu.VMEM((STACK[4], NB), BF16), pltpu.VMEM((STACK[4], NB), BF16),
            pltpu.VMEM((4, NB, NB), BF16), pltpu.VMEM((4, NB, NB), BF16),
            pltpu.VMEM((4, NB, w), F32),
            dma((14,)),
        ],
        compiler_params=pltpu.CompilerParams(vmem_limit_bytes=66_000_000),
        name="solve",
    )(g, ll, lo, b)
    return x, c[None]


def solution(mesh):
    return jax.shard_map(
        per_device,
        mesh=mesh,
        in_specs=(P(None, None, "col", "row"), P(None, "row", "col")),
        out_specs=(P(None, None, "col"), P(None, "row", "col")),
        check_vma=False,
    )
```

time: 248 us -> 132 us (0.53)
  Pallas kernels: 246 us -> 131 us
    pallas_call x1, Pallas kernels: 175 us -> 89.9 us  [per_device(): pl.pallas_call(gather_kernel, out_shape=(jax.ShapeDtypeStruct((4, NB, wid...]
    pallas_call x1, Pallas kernels: 71.1 us -> 40.8 us  [per_device(): pl.pallas_call(solve_kernel, grid=(width // w,), out_shape=(jax.ShapeDtyp...]
where the time goes in v2:
time: 132 us; the launch traced here: 131 us
  Pallas kernels  131 us (99%)
    pallas_call x1, Pallas kernels, per_device(): pl.pallas_call(gather_kernel, out_shape=(jax.ShapeDtypeStruct((4, NB, wid...  89.9 us
    pallas_call x1, Pallas kernels, per_device(): pl.pallas_call(solve_kernel, grid=(width // w,), out_shape=(jax.ShapeDtyp...  40.8 us

profile of v2, /device:TPU:0, one launch (start us, length us, event | category | flops | bytes accessed | tf_op | source)
XLA Modules:
  0.0 131.5 jit_solution(4614779184049857252)
XLA Ops:
  0.6 89.9 %gather.1 = (f32[4,512,1024]{2,1,0:T(8,128)}, f32[4,4,8,64,512]{4,3,2,1,0:T(8,128)}, f32[4,8,64,512]{3,2,1,0:T(8,128)}) custom-call(f32[4,64,512]{2,1,0:T(8,128)} %bitcast.9, f32[512,1024]{1,0:T(8,128)} %bitcast.6), custom_call_target="tpu_custom_call" | custom-call | tf_op jit(solution)/shard_map/gather/pallas_call | solution.py:363
  90.6 40.8 %solve.1 = (f32[4,512,1024]{2,1,0:T(8,128)}, f32[512,1024]{1,0:T(8,128)}) custom-call(f32[4,512,1024]{2,1,0:T(8,128)} %get-tuple-element.7.g, f32[4,4,512,512]{3,2,1,0:T(8,128)} %bitcast.5, f32[4,512,512]{2,1,0:T(8,128)} %bitcast.8, f32[512,1024]{1,0:T(8,128)} %bitcast.7), custom_call_target="tpu_custom_call" | custom-call | tf_op jit(solution)/shard_map/solve/pallas_call | solution.py:382

commit v3 on v2

--- a/solution.py
+++ b/solution.py
@@ -10,9 +10,10 @@
 MESH = pl.DeviceIdType.MESH
 NB = 512
 CW = 128
+HALF = 512
 Z_FIRST = (2, 5, 7)
 N_SEND = 400
-TIMES = (11, 17, 25, 29, 30, 38, 48, 75, 66, 83, 141, 190, 104, 157, 87, 119, 169, 112, 100, 185, 0, 1, 12, 7, 13, 28, 23, 36, 156, 130, 164, 40, 126, 93, 99, 43, 68, 61, 178, 122, 31, 39, 41, 51, 52, 74, 73, 84, 110, 64, 193, 123, 135, 161, 90, 133, 196, 121, 114, 150, 2, 3, 21, 8, 22, 49, 44, 71, 129, 80, 175, 142, 116, 170, 95, 155, 172, 105, 163, 138, 6, 32, 20, 62, 14, 117, 58, 146, 10, 109, 176, 139, 27, 82, 65, 97, 4, 9, 16, 19, 35, 63, 162, 188, 120, 45, 103, 127, 106, 5, 15, 47, 24, 76, 101, 181, 145, 115, 195, 60, 91, 191, 26, 34, 56, 50, 69, 140, 166, 152, 186, 57, 183, 111, 107, 18, 33, 37, 59, 128, 86, 85, 165, 154, 102, 77, 158, 174, 46, 55, 78, 89, 98, 113, 173, 182, 147, 180, 177, 192, 143, 42, 53, 70, 94, 124, 134, 72, 118, 149, 194, 144, 168, 131, 67, 81, 92, 96, 137, 151, 167, 179, 171, 197, 159, 198, 199, 54, 79, 108, 88, 125, 160, 148, 136, 132, 153, 187, 184, 189)
+TIMES = (11, 19, 29, 45, 46, 65, 67, 96, 64, 102, 109, 99, 115, 137, 98, 95, 139, 108, 114, 120, 140, 159, 173, 163, 0, 1, 7, 9, 10, 28, 20, 49, 52, 34, 56, 50, 144, 84, 86, 107, 161, 135, 70, 197, 83, 149, 211, 215, 26, 38, 57, 55, 75, 101, 127, 122, 112, 145, 148, 130, 134, 184, 172, 191, 202, 178, 169, 182, 185, 205, 204, 200, 2, 12, 24, 13, 25, 60, 41, 72, 153, 71, 142, 103, 146, 183, 90, 78, 198, 104, 79, 143, 240, 227, 222, 203, 18, 224, 31, 252, 3, 147, 35, 221, 4, 21, 88, 51, 17, 230, 27, 164, 6, 16, 74, 37, 106, 151, 208, 218, 105, 76, 187, 133, 129, 237, 176, 225, 234, 5, 14, 36, 23, 111, 33, 42, 80, 119, 188, 47, 125, 201, 195, 196, 214, 162, 15, 30, 43, 59, 73, 62, 124, 68, 61, 116, 91, 110, 82, 97, 229, 156, 236, 8, 22, 32, 54, 87, 39, 92, 93, 66, 223, 121, 158, 226, 77, 138, 210, 193, 40, 48, 117, 58, 165, 155, 168, 160, 150, 132, 94, 219, 186, 255, 231, 128, 253, 63, 100, 113, 199, 131, 170, 167, 192, 154, 254, 232, 166, 257, 212, 179, 258, 213, 44, 69, 89, 81, 157, 175, 220, 190, 141, 194, 209, 207, 189, 228, 180, 251, 250, 53, 85, 136, 118, 152, 123, 171, 239, 177, 235, 126, 181, 217, 233, 249, 248, 256, 174, 216, 206, 241, 238, 242, 243, 244, 245, 246, 247, 267, 259, 260, 261, 262, 263, 264, 265, 266)
 F32, BF16 = jnp.float32, jnp.bfloat16
 
 
@@ -23,7 +24,16 @@
         pl.when(cond)(fn)
 
 
-def gather_kernel(lp, b, g, ll, lo, own_sem, gs, sq, sl, sx, st, ox, ot, send):
+def arrange(meta, times):
+    eff = [float(times[i]) if i < len(times) else float(i) for i in range(len(meta))]
+    for i, (_, needs) in enumerate(meta):
+        for j in range(i):
+            if meta[j][0] in needs and eff[j] >= eff[i]:
+                eff[i] = eff[j] + 1e-3
+    return sorted(range(len(meta)), key=lambda i: (eff[i], i))
+
+
+def gather_kernel(lp, b, x_out, lo, g, ll, xb, sh, sw, vh, vw, xh, xl, own_sem, gs, sq, sl, sx, st, ox, ot, send, osem):
     row, col = lax.axis_index("row"), lax.axis_index("col")
     y, z = row // 4, row % 4
     x, core = col // 2, col % 2
@@ -40,8 +50,12 @@
     partner = (row, x * 2 + 1 - core)
     blocks = [(z + d) % 4 for d in (0, 3, 1, 2)]
     OWN, LEFT, RIGHT, OPP = range(4)
-    ops, ends, sends = [], [], []
-    task, last = ops.append, ends.append
+    ops, meta, ends, sends = [], [], [], []
+    last = ends.append
+
+    def task(fn, tag=None, needs=()):
+        ops.append(fn)
+        meta.append((tag, needs))
 
     def put(src, dst, sem, dev, cond=None):
         slot = len(sends)
@@ -69,13 +83,13 @@
     root, other = y == 0, y != 0
 
     def l_ref(blk, k, j=None):
-        return ll.at[blk, blk - k, col if j is None else j]
+        return ll.at[blk * (blk + 1) // 2 + blk - k, col if j is None else j]
 
     def piece(blk, c, q):
         return g.at[blk, pl.ds(pl.multiple_of(q * 128, 128), 128), pl.ds(c * CW, CW)]
 
     def l_quarter(k, q):
-        return ll.at[z, z - k, col, pl.ds(pl.multiple_of(q * 16, 16), 16)]
+        return ll.at[z * (z + 1) // 2 + z - k, col, pl.ds(pl.multiple_of(q * 16, 16), 16)]
 
     for k in range(4):
         when(root & (z >= k), lambda k=k: pltpu.make_async_copy(
@@ -157,16 +171,17 @@
             groups[w][0]()
 
         task(l_scatter)
-        task(l_mine)
-        task(functools.partial(l_relay, -1))
-        task(functools.partial(l_relay, 1))
-        task(l_own)
+        task(l_mine, 30 + k)
+        task(functools.partial(l_relay, -1), 30 + k)
+        task(functools.partial(l_relay, 1), 30 + k)
+        task(l_own, k, (30 + k,))
         for w in (LEFT, RIGHT, OPP):
-            task(functools.partial(l_arrive, w))
+            task(functools.partial(l_arrive, w), k)
         for w in range(4):
             for d in (-1, 1, 2):
-                task(functools.partial(groups[w][1], d, d == (-1 if (k + w) % 2 == 0 else 1)))
-            last(groups[w][2])
+                task(functools.partial(groups[w][1], d, d == (-1 if (k + w) % 2 == 0 else 1)), k)
+        for w in range(4):
+            task(groups[w][2], k)
     for h in range(4):
         start, arrive, done = x_group(lambda j, h=h: lo.at[h, j], ox.at[h], ot.at[h], None, h % 2, src=lp.at[h])
         task(start)
@@ -207,14 +222,27 @@
 
         task(scatter)
         for e in (0, -1, 1, 2):
-            task(functools.partial(first, e))
+            task(functools.partial(first, e), 40 + c // 4)
         for e in (0, -1, 1, 2):
             for d in (-1, 1):
-                task(functools.partial(second, e, d))
-            last(functools.partial(second, e, 2))
-
-    order = sorted(range(len(ops)), key=lambda i: (TIMES[i] if i < len(TIMES) else i, i))
-    for i in order:
+                task(functools.partial(second, e, d), 40 + c // 4)
+        for e in (0, -1, 1, 2):
+            task(functools.partial(second, e, 2), 40 + c // 4)
+
+    task(lambda: do_inverse(ll, vh, vw), 50, (0,))
+    for k in range(1, 4):
+        task(functools.partial(do_prep, k, ll, sh, sw), 51, (k,))
+    for h in range(2):
+        cols = pl.ds(h * HALF, HALF)
+        out = pltpu.make_async_copy(xb.at[:, :, cols], x_out.at[:, :, cols], osem.at[h])
+        for s in range(4):
+            task(functools.partial(do_diag, s, h, g, xb, vh, vw, xh, xl), 60 + 4 * h + s, (50, 40 + h, 69 + 4 * h + s))
+            if s < 3:
+                task(functools.partial(do_stack, s, h, g, xb, sh, sw, xh, xl), 70 + 4 * h + s, (51, 60 + 4 * h + s))
+        task(out.start, None, (63 + 4 * h,))
+        last(out.wait)
+
+    for i in arrange(meta, TIMES):
         ops[i]()
     for fn in ends:
         fn()
@@ -305,54 +333,58 @@
     return out
 
 
-STACK = (0, 2048, 3584, 4608, 5120)
-
-
-def solve_kernel(g, ll, lo, b, x_out, c_out, tiles, sh, sw, vh, vw, acc, sems):
+STACK = (0, 1536, 2560, 3072)
+
+
+def tile_of(ll, r, s):
+    return ll[r * (r + 1) // 2 + s].reshape(NB, NB).T
+
+
+def do_inverse(ll, vh, vw):
+    for s, v in enumerate(invert_tiles([tile_of(ll, s, s) for s in range(4)])):
+        vh[s], vw[s] = split(v)
+
+
+def do_prep(k, ll, sh, sw):
+    for s in range(4 - k):
+        rows = pl.ds(STACK[s] + (k - 1) * NB, NB)
+        sh[rows, :], sw[rows, :] = split(tile_of(ll, s + k, s))
+
+
+def do_diag(s, h, g, xb, vh, vw, xh, xl):
+    cols = pl.ds(h * HALF, HALF)
+    hi, low = split(g[0, :, cols] if s == 0 else xb[s, :, cols])
+    x = dot(vh[s], hi) + (dot(vh[s], low) + dot(vw[s], hi))
+    xb[s, :, cols] = x
+    xh[h], xl[h] = split(x)
+
+
+def do_stack(s, h, g, xb, sh, sw, xh, xl):
+    cols = pl.ds(h * HALF, HALF)
+    rows = pl.ds(STACK[s], STACK[s + 1] - STACK[s])
+    upd = dot(sh[rows, :], xh[h]) + (dot(sh[rows, :], xl[h]) + dot(sw[rows, :], xh[h]))
+    for r in range(s + 1, 4):
+        base = g[r, :, cols] if s == 0 else xb[r, :, cols]
+        xb[r, :, cols] = base - upd[(r - s - 1) * NB:(r - s) * NB]
+
+
+def update_kernel(x, lo, b, x_out, c_out, tiles, oh, ow, sems):
     row = lax.axis_index("row")
 
     @pl.when(pl.program_id(0) == 0)
     def _():
-        wanted = [("d", s, s) for s in range(4)]
-        wanted += [("l", r, s) for s in range(4) for r in range(s + 1, 4)]
-        wanted += [("o", 0, s) for s in range(4)]
-        copies = [
-            pltpu.make_async_copy(lo.at[s] if kind == "o" else ll.at[r, s], tiles.at[n], sems.at[n])
-            for n, (kind, r, s) in enumerate(wanted)
-        ]
+        copies = [pltpu.make_async_copy(lo.at[s], tiles.at[s], sems.at[s]) for s in range(4)]
         for cp in copies:
             cp.start()
-        for cp in copies[:4]:
+        for s, cp in enumerate(copies):
             cp.wait()
-        for s, v in enumerate(invert_tiles([tiles[s].T for s in range(4)])):
-            vh[s], vw[s] = split(v)
-        for n, (kind, r, s) in enumerate(wanted):
-            if n < 4:
-                continue
-            copies[n].wait()
-            t = tiles[n]
-            if kind == "o":
-                t = jnp.where(row > s, t, F32(0.0))
-                rows = pl.ds(STACK[s + 1] - NB, NB)
-            else:
-                rows = pl.ds(STACK[s] + (r - s - 1) * NB, NB)
-            sh[rows, :], sw[rows, :] = split(t.T)
-
-    for s in range(4):
-        hi, low = split(g[0] if s == 0 else acc[s - 1])
-        x = dot(vh[s], hi) + (dot(vh[s], low) + dot(vw[s], hi))
-        x_out[s] = x
-        hi, low = split(x)
-        rows = pl.ds(STACK[s], STACK[s + 1] - STACK[s])
-        upd = dot(sh[rows, :], hi) + (dot(sh[rows, :], low) + dot(sw[rows, :], hi))
-        for r in range(s + 1, 4):
-            base = g[r] if s == 0 else acc[r - 1]
-            acc[r - 1] = base - upd[(r - s - 1) * NB:(r - s) * NB]
-        own = (b[...] if s == 0 else acc[3]) - upd[(3 - s) * NB:]
-        if s == 3:
-            c_out[...] = own
-        else:
-            acc[3] = own
+            cols = pl.ds(s * NB, NB)
+            oh[:, cols], ow[:, cols] = split(jnp.where(row > s, tiles[s], F32(0.0)).T)
+
+    xs = x[...].reshape(4 * NB, x.shape[2])
+    hi, low = split(xs)
+    x_out[...] = x[...]
+    c_out[...] = b[...] - (dot(oh[...], hi) + (dot(oh[...], low) + dot(ow[...], hi)))
 
 
 def per_device(lower_panel, right_side):
@@ -360,44 +392,37 @@
     width = b.shape[1]
     dma = pltpu.SemaphoreType.DMA
     hbm = pl.BlockSpec(memory_space=pl.ANY)
-    g, ll, lo = pl.pallas_call(
+    vm = pltpu.VMEM
+    x, lo = pl.pallas_call(
         gather_kernel,
-        out_shape=(
-            jax.ShapeDtypeStruct((4, NB, width), F32),
-            jax.ShapeDtypeStruct((4, 4, 8, 64, NB), F32),
-            jax.ShapeDtypeStruct((4, 8, 64, NB), F32),
-        ),
+        out_shape=(jax.ShapeDtypeStruct((4, NB, width), F32), jax.ShapeDtypeStruct((4, 8, 64, NB), F32)),
         in_specs=[hbm, hbm],
-        out_specs=(hbm, hbm, hbm),
+        out_specs=(hbm, hbm),
         scratch_shapes=[
+            vm((4, NB, width), F32), vm((10, 8, 64, NB), F32), vm((4, NB, width), F32),
+            vm((STACK[3], NB), BF16), vm((STACK[3], NB), BF16), vm((4, NB, NB), BF16), vm((4, NB, NB), BF16),
+            vm((2, NB, HALF), BF16), vm((2, NB, HALF), BF16),
             dma(()), dma((4, 8, 4)), dma((4, 4)), dma((4, 4)), dma((4, 4, 4)), dma((4, 4, 4)),
-            dma((4, 4)), dma((4, 4)), dma((N_SEND,)),
+            dma((4, 4)), dma((4, 4)), dma((N_SEND,)), dma((2,)),
         ],
-        compiler_params=pltpu.CompilerParams(collective_id=0, has_side_effects=True),
+        compiler_params=pltpu.CompilerParams(
+            collective_id=0, has_side_effects=True, vmem_limit_bytes=66_000_000),
         name="gather",
     )(lp, b)
-    ll = ll.reshape(4, 4, NB, NB)
     lo = lo.reshape(4, NB, NB)
     w = 512
     x, c = pl.pallas_call(
-        solve_kernel,
+        update_kernel,
         grid=(width // w,),
         out_shape=(jax.ShapeDtypeStruct((4, NB, width), F32), jax.ShapeDtypeStruct((NB, width), F32)),
         in_specs=[
-            pl.BlockSpec((4, NB, w), lambda i: (0, 0, i)), hbm, hbm,
-            pl.BlockSpec((NB, w), lambda i: (0, i)),
+            pl.BlockSpec((4, NB, w), lambda i: (0, 0, i)), hbm, pl.BlockSpec((NB, w), lambda i: (0, i)),
         ],
         out_specs=(pl.BlockSpec((4, NB, w), lambda i: (0, 0, i)), pl.BlockSpec((NB, w), lambda i: (0, i))),
-        scratch_shapes=[
-            pltpu.VMEM((14, NB, NB), F32),
-            pltpu.VMEM((STACK[4], NB), BF16), pltpu.VMEM((STACK[4], NB), BF16),
-            pltpu.VMEM((4, NB, NB), BF16), pltpu.VMEM((4, NB, NB), BF16),
-            pltpu.VMEM((4, NB, w), F32),
-            dma((14,)),
-        ],
-        compiler_params=pltpu.CompilerParams(vmem_limit_bytes=66_000_000),
-        name="solve",
-    )(g, ll, lo, b)
+        scratch_shapes=[vm((4, NB, NB), F32), vm((NB, 4 * NB), BF16), vm((NB, 4 * NB), BF16), dma((4,))],
+        compiler_params=pltpu.CompilerParams(vmem_limit_bytes=60_000_000),
+        name="update",
+    )(x, lo, b)
     return x, c[None]
 
 

time: 132 us -> 127 us (0.962)
  Pallas kernels: 131 us -> 125 us
    pallas_call x1, Pallas kernels: 40.8 us -> 14.1 us  [per_device(): pl.pallas_call(update_kernel, grid=(width // w,), out_shape=(jax.ShapeDty...]
    pallas_call x1, Pallas kernels: 89.9 us -> 111 us  [per_device(): pl.pallas_call(gather_kernel, out_shape=(jax.ShapeDtypeStruct((4, NB, wid...]
where the time goes in v3:
time: 127 us; the launch traced here: 126 us
  Pallas kernels  125 us (98%)
    pallas_call x1, Pallas kernels, per_device(): pl.pallas_call(gather_kernel, out_shape=(jax.ShapeDtypeStruct((4, NB, wid...  111 us
    pallas_call x1, Pallas kernels, per_device(): pl.pallas_call(update_kernel, grid=(width // w,), out_shape=(jax.ShapeDty...  14.1 us

profile of v3, /device:TPU:0, one launch (start us, length us, event | category | flops | bytes accessed | tf_op | source)
XLA Modules:
  0.0 126.2 jit_solution(13765093771864093246)
XLA Ops:
  0.6 111.2 %gather.1 = (f32[4,512,1024]{2,1,0:T(8,128)}, f32[4,8,64,512]{3,2,1,0:T(8,128)}) custom-call(f32[4,64,512]{2,1,0:T(8,128)} %bitcast.7, f32[512,1024]{1,0:T(8,128)} %bitcast.4), custom_call_target="tpu_custom_call" | custom-call | tf_op jit(solution)/shard_map/gather/pallas_call | solution.py:396
  111.8 14.1 %update.1 = (f32[4,512,1024]{2,1,0:T(8,128)}, f32[512,1024]{1,0:T(8,128)}) custom-call(f32[4,512,1024]{2,1,0:T(8,128)} %get-tuple-element.6.x, f32[4,512,512]{2,1,0:T(8,128)} %bitcast.6, f32[512,1024]{1,0:T(8,128)} %bitcast.5), custom_call_target="tpu_custom_call" | custom-call | tf_op jit(solution)/shard_map/update/pallas_call | solution.py:414

commit v4 on v3

--- a/solution.py
+++ b/solution.py
@@ -11,9 +11,11 @@
 NB = 512
 CW = 128
 HALF = 512
-Z_FIRST = (2, 5, 7)
+Z_FIRST = (1, 3, 5, 7)
+Y_PLUS = (0,)
+E_PLUS = (0,)
 N_SEND = 400
-TIMES = (11, 19, 29, 45, 46, 65, 67, 96, 64, 102, 109, 99, 115, 137, 98, 95, 139, 108, 114, 120, 140, 159, 173, 163, 0, 1, 7, 9, 10, 28, 20, 49, 52, 34, 56, 50, 144, 84, 86, 107, 161, 135, 70, 197, 83, 149, 211, 215, 26, 38, 57, 55, 75, 101, 127, 122, 112, 145, 148, 130, 134, 184, 172, 191, 202, 178, 169, 182, 185, 205, 204, 200, 2, 12, 24, 13, 25, 60, 41, 72, 153, 71, 142, 103, 146, 183, 90, 78, 198, 104, 79, 143, 240, 227, 222, 203, 18, 224, 31, 252, 3, 147, 35, 221, 4, 21, 88, 51, 17, 230, 27, 164, 6, 16, 74, 37, 106, 151, 208, 218, 105, 76, 187, 133, 129, 237, 176, 225, 234, 5, 14, 36, 23, 111, 33, 42, 80, 119, 188, 47, 125, 201, 195, 196, 214, 162, 15, 30, 43, 59, 73, 62, 124, 68, 61, 116, 91, 110, 82, 97, 229, 156, 236, 8, 22, 32, 54, 87, 39, 92, 93, 66, 223, 121, 158, 226, 77, 138, 210, 193, 40, 48, 117, 58, 165, 155, 168, 160, 150, 132, 94, 219, 186, 255, 231, 128, 253, 63, 100, 113, 199, 131, 170, 167, 192, 154, 254, 232, 166, 257, 212, 179, 258, 213, 44, 69, 89, 81, 157, 175, 220, 190, 141, 194, 209, 207, 189, 228, 180, 251, 250, 53, 85, 136, 118, 152, 123, 171, 239, 177, 235, 126, 181, 217, 233, 249, 248, 256, 174, 216, 206, 241, 238, 242, 243, 244, 245, 246, 247, 267, 259, 260, 261, 262, 263, 264, 265, 266)
+TIMES = (0, 3, 6, 14, 15, 20, 26, 31, 39, 90, 57, 113, 114, 36, 62, 49, 70, 71, 51, 69, 80, 91, 108, 32, 43, 42, 78, 79, 4, 11, 23, 18, 24, 52, 40, 50, 53, 74, 153, 119, 154, 54, 94, 131, 164, 183, 55, 96, 132, 157, 158, 2, 12, 21, 47, 48, 63, 100, 99, 101, 128, 155, 178, 185, 102, 135, 126, 151, 169, 7, 25, 41, 28, 45, 75, 67, 104, 105, 145, 177, 205, 214, 10, 165, 77, 233, 17, 133, 142, 191, 5, 22, 88, 68, 1, 87, 9, 37, 8, 30, 59, 85, 110, 106, 66, 130, 148, 159, 150, 156, 136, 168, 203, 188, 211, 16, 33, 46, 76, 103, 122, 175, 118, 72, 173, 111, 193, 146, 199, 139, 207, 206, 19, 44, 83, 93, 121, 95, 120, 134, 112, 187, 162, 166, 200, 210, 152, 201, 212, 13, 38, 60, 56, 84, 81, 149, 124, 109, 141, 61, 176, 123, 172, 147, 208, 161, 27, 58, 196, 64, 86, 197, 82, 239, 220, 97, 202, 179, 117, 234, 243, 246, 221, 35, 92, 137, 144, 180, 181, 140, 192, 198, 217, 223, 241, 219, 238, 247, 236, 240, 29, 65, 129, 98, 167, 182, 194, 160, 209, 143, 125, 222, 235, 225, 244, 170, 237, 34, 73, 107, 89, 138, 163, 189, 195, 171, 190, 174, 224, 204, 232, 218, 245, 242, 115, 116, 127, 184, 186, 215, 213, 216, 226, 227, 228, 229, 230, 231, 248, 249, 250, 251, 252, 253, 254, 255)
 F32, BF16 = jnp.float32, jnp.bfloat16
 
 
@@ -33,7 +35,7 @@
     return sorted(range(len(meta)), key=lambda i: (eff[i], i))
 
 
-def gather_kernel(lp, b, x_out, lo, g, ll, xb, sh, sw, vh, vw, xh, xl, own_sem, gs, sq, sl, sx, st, ox, ot, send, osem):
+def gather_kernel(lp, b, x_out, lo, g, ll, xb, sh, sw, vh, vw, xh, xl, tl, iv, ir, own_sem, gs, sq, sl, sx, st, ox, ot, send, osem):
     row, col = lax.axis_index("row"), lax.axis_index("col")
     y, z = row // 4, row % 4
     x, core = col // 2, col % 2
@@ -103,38 +105,43 @@
 
     pl.semaphore_wait(barrier, len(around))
 
-    def x_group(ref_of, xs, ts, cond, parity, src=None):
-        def j_of(xx, cc):
-            return xx * 2 + cc
+    def x_group(ref_of, xs, ts, cond, src=None, halved=False):
+        def parts(xx, cc, src=None):
+            r = ref_of(xx * 2 + cc)
+            f = r if src is None else src
+            if not halved:
+                return [(cond, f, r)]
+            low, high = xx < 2, xx >= 2
+            if cond is not None:
+                low, high = low & cond, high & cond
+            tail = pl.ds(NB // 2, NB // 2)
+            return [(low, f, r), (high, f.at[:, tail], r.at[:, tail])]
 
         def start():
-            s = ref_of(col) if src is None else src
-            d = ref_of(col)
-            put(s, d, xs.at[x], x_dev(1), cond)
-            put(s, d, xs.at[x], x_dev(-1), cond)
-            put(s, d, ts.at[x], partner, cond)
+            for on, f, r in parts(x, core, src):
+                put(f, r, xs.at[x], x_dev(1), on)
+                put(f, r, xs.at[x], x_dev(-1), on)
+                put(f, r, ts.at[x], partner, on)
 
         def arrive(d, relay):
             xx = (x + d + 4) % 4
-            r = ref_of(j_of(xx, core))
-            got(r, xs.at[xx], cond)
-            if relay:
-                put(r, r, xs.at[xx], x_dev(-d), cond)
-            put(r, r, ts.at[xx], partner, cond)
+            for on, _, r in parts(xx, core):
+                got(r, xs.at[xx], on)
+                if relay:
+                    put(r, r, xs.at[xx], x_dev(-d), on)
+                put(r, r, ts.at[xx], partner, on)
 
         def done():
             for xx in range(4):
-                got(ref_of(j_of(xx, 1 - core)), ts.at[xx], cond)
+                r, on = ref_of(xx * 2 + 1 - core), cond
+                if halved and xx >= 2:
+                    r = r.at[:, pl.ds(NB // 2, NB // 2)]
+                got(r, ts.at[xx], on)
 
         return start, arrive, done
 
     for k in range(4):
         conds = [None if k == 0 else blk >= k for blk in blocks]
-        groups = [
-            x_group(lambda j, blk=blocks[w], k=k: l_ref(blk, k, j), sx.at[blocks[w], k], st.at[blocks[w], k],
-                    conds[w], (k + w) % 2)
-            for w in range(4)
-        ]
 
         def l_scatter(k=k, cond=conds[OWN]):
             for q in (1, 3, 2):
@@ -154,39 +161,41 @@
             if d == (-1 if k % 2 == 0 else 1):
                 put(r, r, sem, y_dev(-d), cond)
 
-        def l_own(k=k, cond=conds[OWN], start=groups[OWN][0]):
+        def l_own(k=k, cond=conds[OWN]):
             q = (y + 2) % 4
             got(l_quarter(k, q), sq.at[k, q], cond)
             r, sem = l_ref(z, k), sl.at[z, k]
             put(r, r, sem, z_dev(1), cond)
             put(r, r, sem, z_dev(-1), cond)
-            start()
-
-        def l_arrive(w, k=k, conds=conds, groups=groups):
+
+        def l_arrive(w, k=k, conds=conds):
             blk, cond = blocks[w], conds[w]
             r, sem = l_ref(blk, k), sl.at[blk, k]
             got(r, sem, cond)
             if w == (LEFT if k % 2 == 0 else RIGHT):
                 put(r, r, sem, z_dev(1 if w == LEFT else -1), cond)
-            groups[w][0]()
 
         task(l_scatter)
-        task(l_mine, 30 + k)
-        task(functools.partial(l_relay, -1), 30 + k)
-        task(functools.partial(l_relay, 1), 30 + k)
-        task(l_own, k, (30 + k,))
+        task(l_mine, 34 + k)
+        task(functools.partial(l_relay, -1), 34 + k)
+        task(functools.partial(l_relay, 1), 34 + k)
+        task(l_own, 30 + k, (34 + k,))
         for w in (LEFT, RIGHT, OPP):
-            task(functools.partial(l_arrive, w), k)
-        for w in range(4):
+            task(functools.partial(l_arrive, w), 30 + k)
+        for blk in range(k, 4):
+            start, arrive, done = x_group(
+                lambda j, blk=blk, k=k: l_ref(blk, k, j), sx.at[blk, k], st.at[blk, k], None, None, k == 0)
+            unit = 100 + 4 * k + blk
+            task(start, unit, (30 + k,))
             for d in (-1, 1, 2):
-                task(functools.partial(groups[w][1], d, d == (-1 if (k + w) % 2 == 0 else 1)), k)
-        for w in range(4):
-            task(groups[w][2], k)
+                task(functools.partial(arrive, d, d == (-1 if (k + blk) % 2 == 0 else 1)), 20 + unit, (unit,))
+            task(done, k, (20 + unit,))
+
     for h in range(4):
-        start, arrive, done = x_group(lambda j, h=h: lo.at[h, j], ox.at[h], ot.at[h], None, h % 2, src=lp.at[h])
-        task(start)
+        start, arrive, done = x_group(lambda j, h=h: lo.at[h, j], ox.at[h], ot.at[h], None, lp.at[h])
+        task(start, 90 + h)
         for d in (-1, 1, 2):
-            task(functools.partial(arrive, d, d == (-1 if h % 2 == 0 else 1)))
+            task(functools.partial(arrive, d, d == (-1 if h % 2 == 0 else 1)), 90 + h)
         last(done)
 
     for c in range(8):
@@ -203,21 +212,21 @@
             blk, q = (i1, i2) if zfirst else (i2, i1)
             return piece(blk, c, q), gs.at[blk, c, q]
 
-        def first(e, c=c, at=at, dev1=dev1, dev2=dev2):
+        def first(e, c=c, at=at, dev1=dev1, dev2=dev2, zfirst=zfirst):
             r, sem = at(e, 0)
             got(r, sem)
             if e == 0:
                 put(r, r, sem, dev1(1))
                 put(r, r, sem, dev1(-1))
-            elif e == (-1 if c // 2 % 2 == 0 else 1):
+            elif e == (-1 if (c // 2 % 2 == 0 if zfirst else c in Y_PLUS) else 1):
                 put(r, r, sem, dev1(-e))
             put(r, r, sem, dev2(1))
             put(r, r, sem, dev2(-1))
 
-        def second(e, d, at=at, dev2=dev2):
+        def second(e, d, at=at, dev2=dev2, zfirst=zfirst):
             r, sem = at(e, d)
             got(r, sem)
-            if d == (-1 if e in (0, 2) else 1):
+            if d == (-1 if e in (E_PLUS if zfirst else (0, 2)) else 1):
                 put(r, r, sem, dev2(-d))
 
         task(scatter)
@@ -229,7 +238,9 @@
         for e in (0, -1, 1, 2):
             task(functools.partial(second, e, 2), 40 + c // 4)
 
-    task(lambda: do_inverse(ll, vh, vw), 50, (0,))
+    task(lambda: do_inverse_base(ll, tl, iv, ir), 48, (0,))
+    task(lambda: do_inverse_blocks(tl, iv), 49, (48,))
+    task(lambda: do_inverse_join(tl, iv, ir, vh, vw), 50, (49,))
     for k in range(1, 4):
         task(functools.partial(do_prep, k, ll, sh, sw), 51, (k,))
     for h in range(2):
@@ -272,65 +283,72 @@
     return dot(ah, bh) + (dot(ah, bl) + dot(al, bh))
 
 
-def invert_tiles(tiles):
-    n = 128
-    ri = lax.broadcasted_iota(jnp.int32, (n, n), 0)
-    ci = lax.broadcasted_iota(jnp.int32, (n, n), 1)
+def block_iotas():
+    ri = lax.broadcasted_iota(jnp.int32, (CW, CW), 0)
+    return ri, lax.broadcasted_iota(jnp.int32, (CW, CW), 1)
+
+
+def strict_block(tl, i):
+    ri, ci = block_iotas()
+    rows = pl.ds(i % 4 * CW, CW)
+    return jnp.where(ri > ci, tl[i // 4, rows, rows], F32(0.0))
+
+
+def do_inverse_base(ll, tl, iv, ir):
+    ri, ci = block_iotas()
     eye = ri == ci
+    for s in range(4):
+        t = tile_of(ll, s, s)
+        for d in range(4):
+            rows = pl.ds(d * CW, CW)
+            diag = jnp.where(eye, t[d * CW:(d + 1) * CW, d * CW:(d + 1) * CW], F32(0.0))
+            tl[s, rows, :] = t[d * CW:(d + 1) * CW] * (F32(1.0) / jnp.sum(diag, axis=1, keepdims=True))
+            ir[s, :, rows] = F32(1.0) / jnp.sum(diag, axis=0, keepdims=True)
     ident = jnp.where(eye, F32(1.0), F32(0.0))
-    count = len(tiles)
-    scaled, inv_row, parts = [], [], []
-    for t in tiles:
-        cols, rows = [], []
-        for d in range(4):
-            blk = t[d * n:(d + 1) * n, d * n:(d + 1) * n]
-            diag = jnp.where(eye, blk, F32(0.0))
-            cols.append(F32(1.0) / jnp.sum(diag, axis=1, keepdims=True))
-            rows.append(F32(1.0) / jnp.sum(diag, axis=0, keepdims=True))
-        scaled.append([[t[a * n:(a + 1) * n, c * n:(c + 1) * n] * cols[a] for c in range(a + 1)] for a in range(4)])
-        inv_row.append(jnp.concatenate(rows, axis=1))
-    for t in scaled:
-        for d in range(4):
-            parts.append(jnp.where(ri > ci, t[d][d], F32(0.0)))
     same8 = (ri // 8) == (ci // 8)
-    small = [jnp.where(same8, p, F32(0.0)) for p in parts]
+    small = [jnp.where(same8, strict_block(tl, i), F32(0.0)) for i in range(16)]
     sq = [dot_small(m, m) for m in small]
     inv = [(ident - m) for m in small]
     step = [dot_small(v, q) for v, q in zip(inv, sq)]
     quad = [dot_small(q, q) for q in sq]
     inv = [v + s for v, s in zip(inv, step)]
     step = [dot_small(v, q) for v, q in zip(inv, quad)]
-    inv = [v + s for v, s in zip(inv, step)]
+    for i in range(16):
+        iv[i] = inv[i] + step[i]
+
+
+def do_inverse_blocks(tl, iv):
+    ri, ci = block_iotas()
+    inv = [iv[i] for i in range(16)]
     for w in (8, 16, 32, 64):
         mask = (ri // (2 * w) == ci // (2 * w)) & ((ri // w) != (ci // w))
-        low = [dot_small(jnp.where(mask, p, F32(0.0)), v) for p, v in zip(parts, inv)]
+        low = [dot_small(jnp.where(mask, strict_block(tl, i), F32(0.0)), v) for i, v in enumerate(inv)]
         step = [dot_small(v, s) for v, s in zip(inv, low)]
         inv = [v - s for v, s in zip(inv, step)]
-    zero = jnp.zeros((n, n), F32)
+    for i in range(16):
+        iv[i] = inv[i]
+
+
+def do_inverse_join(tl, iv, ir, vh, vw):
+    zero = jnp.zeros((CW, CW), F32)
     pairs, low = [], []
-    for k in range(count):
+    for k in range(4):
         for h in range(2):
-            low.append(dot_small(scaled[k][2 * h + 1][2 * h], inv[4 * k + 2 * h]))
-    for k in range(count):
+            rows, cols = pl.ds((2 * h + 1) * CW, CW), pl.ds(2 * h * CW, CW)
+            low.append(dot_small(tl[k, rows, cols], iv[4 * k + 2 * h]))
+    for k in range(4):
         for h in range(2):
-            a, c = inv[4 * k + 2 * h], inv[4 * k + 2 * h + 1]
+            a, c = iv[4 * k + 2 * h], iv[4 * k + 2 * h + 1]
             e = -dot_small(c, low[2 * k + h])
             pairs.append(jnp.concatenate(
                 [jnp.concatenate([a, zero], axis=1), jnp.concatenate([e, c], axis=1)], axis=0))
-    low = []
-    for k in range(count):
-        t = scaled[k]
-        corner = jnp.concatenate(
-            [jnp.concatenate(t[2][:2], axis=1), jnp.concatenate(t[3][:2], axis=1)], axis=0)
-        low.append(dot3(corner, pairs[2 * k]))
+    low = [dot3(tl[k, pl.ds(256, 256), pl.ds(0, 256)], pairs[2 * k]) for k in range(4)]
     zero = jnp.zeros((256, 256), F32)
-    out = []
-    for k in range(count):
+    for k in range(4):
         e = -dot3(pairs[2 * k + 1], low[k])
         full = jnp.concatenate(
             [jnp.concatenate([pairs[2 * k], zero], axis=1), jnp.concatenate([e, pairs[2 * k + 1]], axis=1)], axis=0)
-        out.append(full * inv_row[k])
-    return out
+        vh[k], vw[k] = split(full * ir[k])
 
 
 STACK = (0, 1536, 2560, 3072)
@@ -338,11 +356,6 @@
 
 def tile_of(ll, r, s):
     return ll[r * (r + 1) // 2 + s].reshape(NB, NB).T
-
-
-def do_inverse(ll, vh, vw):
-    for s, v in enumerate(invert_tiles([tile_of(ll, s, s) for s in range(4)])):
-        vh[s], vw[s] = split(v)
 
 
 def do_prep(k, ll, sh, sw):
@@ -402,6 +415,7 @@
             vm((4, NB, width), F32), vm((10, 8, 64, NB), F32), vm((4, NB, width), F32),
             vm((STACK[3], NB), BF16), vm((STACK[3], NB), BF16), vm((4, NB, NB), BF16), vm((4, NB, NB), BF16),
             vm((2, NB, HALF), BF16), vm((2, NB, HALF), BF16),
+            vm((4, NB, NB), F32), vm((16, CW, CW), F32), vm((4, 1, NB), F32),
             dma(()), dma((4, 8, 4)), dma((4, 4)), dma((4, 4)), dma((4, 4, 4)), dma((4, 4, 4)),
             dma((4, 4)), dma((4, 4)), dma((N_SEND,)), dma((2,)),
         ],

time: 127 us -> 115 us (0.906)
  Pallas kernels: 125 us -> 114 us
    pallas_call x1, Pallas kernels: 111 us -> 99.6 us  [per_device(): pl.pallas_call(gather_kernel, out_shape=(jax.ShapeDtypeStruct((4, NB, wid...]
where the time goes in v4:
time: 115 us
  Pallas kernels  114 us (99%)
    pallas_call x1, Pallas kernels, per_device(): pl.pallas_call(gather_kernel, out_shape=(jax.ShapeDtypeStruct((4, NB, wid...  99.6 us
    pallas_call x1, Pallas kernels, per_device(): pl.pallas_call(update_kernel, grid=(width // w,), out_shape=(jax.ShapeDty...  14.1 us

profile of v4, /device:TPU:0, one launch (start us, length us, event | category | flops | bytes accessed | tf_op | source)
XLA Modules:
  0.0 114.5 jit_solution(7908171372215933796)
XLA Ops:
  0.6 99.6 %gather.1 = (f32[4,512,1024]{2,1,0:T(8,128)}, f32[4,8,64,512]{3,2,1,0:T(8,128)}) custom-call(f32[4,64,512]{2,1,0:T(8,128)} %bitcast.7, f32[512,1024]{1,0:T(8,128)} %bitcast.4), custom_call_target="tpu_custom_call" | custom-call | tf_op jit(solution)/shard_map/gather/pallas_call | solution.py:409
  100.2 14.1 %update.1 = (f32[4,512,1024]{2,1,0:T(8,128)}, f32[512,1024]{1,0:T(8,128)}) custom-call(f32[4,512,1024]{2,1,0:T(8,128)} %get-tuple-element.6.x, f32[4,512,512]{2,1,0:T(8,128)} %bitcast.6, f32[512,1024]{1,0:T(8,128)} %bitcast.5), custom_call_target="tpu_custom_call" | custom-call | tf_op jit(solution)/shard_map/update/pallas_call | solution.py:428

commit v5 on v4

--- a/solution.py
+++ b/solution.py
@@ -15,7 +15,7 @@
 Y_PLUS = (0,)
 E_PLUS = (0,)
 N_SEND = 400
-TIMES = (0, 3, 6, 14, 15, 20, 26, 31, 39, 90, 57, 113, 114, 36, 62, 49, 70, 71, 51, 69, 80, 91, 108, 32, 43, 42, 78, 79, 4, 11, 23, 18, 24, 52, 40, 50, 53, 74, 153, 119, 154, 54, 94, 131, 164, 183, 55, 96, 132, 157, 158, 2, 12, 21, 47, 48, 63, 100, 99, 101, 128, 155, 178, 185, 102, 135, 126, 151, 169, 7, 25, 41, 28, 45, 75, 67, 104, 105, 145, 177, 205, 214, 10, 165, 77, 233, 17, 133, 142, 191, 5, 22, 88, 68, 1, 87, 9, 37, 8, 30, 59, 85, 110, 106, 66, 130, 148, 159, 150, 156, 136, 168, 203, 188, 211, 16, 33, 46, 76, 103, 122, 175, 118, 72, 173, 111, 193, 146, 199, 139, 207, 206, 19, 44, 83, 93, 121, 95, 120, 134, 112, 187, 162, 166, 200, 210, 152, 201, 212, 13, 38, 60, 56, 84, 81, 149, 124, 109, 141, 61, 176, 123, 172, 147, 208, 161, 27, 58, 196, 64, 86, 197, 82, 239, 220, 97, 202, 179, 117, 234, 243, 246, 221, 35, 92, 137, 144, 180, 181, 140, 192, 198, 217, 223, 241, 219, 238, 247, 236, 240, 29, 65, 129, 98, 167, 182, 194, 160, 209, 143, 125, 222, 235, 225, 244, 170, 237, 34, 73, 107, 89, 138, 163, 189, 195, 171, 190, 174, 224, 204, 232, 218, 245, 242, 115, 116, 127, 184, 186, 215, 213, 216, 226, 227, 228, 229, 230, 231, 248, 249, 250, 251, 252, 253, 254, 255)
+TIMES = (0, 6, 9, 14, 22, 28, 34, 44, 45, 63, 59, 110, 115, 46, 70, 71, 99, 105, 47, 79, 80, 100, 109, 48, 85, 86, 114, 124, 7, 17, 37, 24, 38, 68, 62, 87, 88, 117, 135, 162, 169, 89, 132, 138, 183, 193, 90, 133, 148, 180, 181, 3, 8, 12, 18, 30, 56, 50, 92, 93, 146, 173, 201, 206, 94, 156, 165, 202, 203, 11, 29, 74, 40, 75, 136, 98, 126, 137, 185, 179, 215, 221, 1, 15, 13, 42, 4, 25, 26, 43, 2, 19, 21, 53, 5, 33, 32, 55, 10, 27, 64, 52, 128, 41, 49, 103, 96, 84, 67, 175, 167, 82, 123, 97, 217, 20, 51, 73, 60, 111, 108, 61, 145, 116, 121, 81, 177, 152, 168, 176, 120, 170, 23, 54, 101, 91, 119, 83, 69, 154, 127, 134, 118, 163, 158, 130, 166, 172, 195, 16, 35, 66, 57, 76, 77, 58, 140, 95, 104, 72, 151, 106, 161, 143, 122, 139, 31, 78, 171, 102, 131, 142, 107, 210, 197, 150, 129, 174, 186, 187, 220, 188, 213, 36, 112, 155, 153, 189, 178, 147, 214, 190, 209, 191, 226, 208, 237, 233, 229, 234, 65, 141, 184, 182, 204, 212, 200, 228, 211, 235, 205, 232, 225, 245, 230, 236, 247, 39, 113, 159, 149, 192, 199, 157, 219, 216, 196, 164, 231, 227, 246, 244, 198, 243, 125, 144, 160, 194, 207, 222, 218, 223, 224, 238, 239, 240, 241, 242, 248, 249, 250, 251, 252, 253, 254, 255)
 F32, BF16 = jnp.float32, jnp.bfloat16
 
 
@@ -381,23 +381,38 @@
         xb[r, :, cols] = base - upd[(r - s - 1) * NB:(r - s) * NB]
 
 
-def update_kernel(x, lo, b, x_out, c_out, tiles, oh, ow, sems):
+def update_kernel(x, lo, b, x_out, c_out, xv, bv, cv, tiles, oh, ow, in_sem, out_sem, lo_sem, b_sem):
     row = lax.axis_index("row")
-
-    @pl.when(pl.program_id(0) == 0)
-    def _():
-        copies = [pltpu.make_async_copy(lo.at[s], tiles.at[s], sems.at[s]) for s in range(4)]
-        for cp in copies:
-            cp.start()
-        for s, cp in enumerate(copies):
-            cp.wait()
+    halves = [pl.ds(h * HALF, HALF) for h in range(2)]
+    loads = [pltpu.make_async_copy(lo.at[s], tiles.at[s], lo_sem.at[s]) for s in range(4)]
+    ins = [[pltpu.make_async_copy(x.at[s, :, c], xv.at[h, s], in_sem.at[h, s]) for s in range(4)] for h, c in enumerate(halves)]
+    outs = [[pltpu.make_async_copy(xv.at[h, s], x_out.at[s, :, c], out_sem.at[h, s]) for s in range(4)]
+            for h, c in enumerate(halves)]
+    rhs = [pltpu.make_async_copy(b.at[:, c], bv.at[h], b_sem.at[h]) for h, c in enumerate(halves)]
+    res = [pltpu.make_async_copy(cv.at[h], c_out.at[:, c], b_sem.at[2 + h]) for h, c in enumerate(halves)]
+    for s in range(4):
+        loads[s].start()
+        ins[0][s].start()
+        if s == 0:
+            rhs[0].start()
+    for cp in ins[1] + rhs[1:]:
+        cp.start()
+    for h in range(2):
+        for s in range(4):
             cols = pl.ds(s * NB, NB)
-            oh[:, cols], ow[:, cols] = split(jnp.where(row > s, tiles[s], F32(0.0)).T)
-
-    xs = x[...].reshape(4 * NB, x.shape[2])
-    hi, low = split(xs)
-    x_out[...] = x[...]
-    c_out[...] = b[...] - (dot(oh[...], hi) + (dot(oh[...], low) + dot(ow[...], hi)))
+            if h == 0:
+                loads[s].wait()
+                oh[:, cols], ow[:, cols] = split(jnp.where(row > s, tiles[s], F32(0.0)).T)
+            ins[h][s].wait()
+            outs[h][s].start()
+            hi, low = split(xv[h, s])
+            upd = dot(oh[:, cols], hi) + (dot(oh[:, cols], low) + dot(ow[:, cols], hi))
+            if s == 0:
+                rhs[h].wait()
+            cv[h] = (bv[h] if s == 0 else cv[h]) - upd
+        res[h].start()
+    for cp in outs[0] + outs[1] + res:
+        cp.wait()
 
 
 def per_device(lower_panel, right_side):
@@ -424,16 +439,16 @@
         name="gather",
     )(lp, b)
     lo = lo.reshape(4, NB, NB)
-    w = 512
     x, c = pl.pallas_call(
         update_kernel,
-        grid=(width // w,),
         out_shape=(jax.ShapeDtypeStruct((4, NB, width), F32), jax.ShapeDtypeStruct((NB, width), F32)),
-        in_specs=[
-            pl.BlockSpec((4, NB, w), lambda i: (0, 0, i)), hbm, pl.BlockSpec((NB, w), lambda i: (0, i)),
+        in_specs=[hbm, hbm, hbm],
+        out_specs=(hbm, hbm),
+        scratch_shapes=[
+            vm((2, 4, NB, HALF), F32), vm((2, NB, HALF), F32), vm((2, NB, HALF), F32), vm((4, NB, NB), F32),
+            vm((NB, 4 * NB), BF16), vm((NB, 4 * NB), BF16),
+            dma((2, 4)), dma((2, 4)), dma((4,)), dma((4,)),
         ],
-        out_specs=(pl.BlockSpec((4, NB, w), lambda i: (0, 0, i)), pl.BlockSpec((NB, w), lambda i: (0, i))),
-        scratch_shapes=[vm((4, NB, NB), F32), vm((NB, 4 * NB), BF16), vm((NB, 4 * NB), BF16), dma((4,))],
         compiler_params=pltpu.CompilerParams(vmem_limit_bytes=60_000_000),
         name="update",
     )(x, lo, b)

time: 115 us -> 113 us (0.983)
  Pallas kernels: 114 us -> 112 us
where the time goes in v5:
time: 113 us
  Pallas kernels  112 us (99%)
    pallas_call x1, Pallas kernels, per_device(): pl.pallas_call(gather_kernel, out_shape=(jax.ShapeDtypeStruct((4, NB, wid...  98.8 us
    pallas_call x1, Pallas kernels, per_device(): pl.pallas_call(update_kernel, out_shape=(jax.ShapeDtypeStruct((4, NB, wid...  13.3 us

profile of v5, /device:TPU:0, one launch (start us, length us, event | category | flops | bytes accessed | tf_op | source)
XLA Modules:
  0.0 112.9 jit_solution(8519682153414870409)
XLA Ops:
  0.6 98.8 %gather.1 = (f32[4,512,1024]{2,1,0:T(8,128)}, f32[4,8,64,512]{3,2,1,0:T(8,128)}) custom-call(f32[4,64,512]{2,1,0:T(8,128)} %bitcast.7, f32[512,1024]{1,0:T(8,128)} %bitcast.4), custom_call_target="tpu_custom_call" | custom-call | tf_op jit(solution)/shard_map/gather/pallas_call | solution.py:424
  99.4 13.3 %update.1 = (f32[4,512,1024]{2,1,0:T(8,128)}, f32[512,1024]{1,0:T(8,128)}) custom-call(f32[4,512,1024]{2,1,0:T(8,128)} %get-tuple-element.6.x, f32[4,512,512]{2,1,0:T(8,128)} %bitcast.6, f32[512,1024]{1,0:T(8,128)} %bitcast.5), custom_call_target="tpu_custom_call" | custom-call | tf_op jit(solution)/shard_map/update/pallas_call | solution.py:442

commit v6 on v5

--- a/solution.py
+++ b/solution.py
@@ -15,7 +15,7 @@
 Y_PLUS = (0,)
 E_PLUS = (0,)
 N_SEND = 400
-TIMES = (0, 6, 9, 14, 22, 28, 34, 44, 45, 63, 59, 110, 115, 46, 70, 71, 99, 105, 47, 79, 80, 100, 109, 48, 85, 86, 114, 124, 7, 17, 37, 24, 38, 68, 62, 87, 88, 117, 135, 162, 169, 89, 132, 138, 183, 193, 90, 133, 148, 180, 181, 3, 8, 12, 18, 30, 56, 50, 92, 93, 146, 173, 201, 206, 94, 156, 165, 202, 203, 11, 29, 74, 40, 75, 136, 98, 126, 137, 185, 179, 215, 221, 1, 15, 13, 42, 4, 25, 26, 43, 2, 19, 21, 53, 5, 33, 32, 55, 10, 27, 64, 52, 128, 41, 49, 103, 96, 84, 67, 175, 167, 82, 123, 97, 217, 20, 51, 73, 60, 111, 108, 61, 145, 116, 121, 81, 177, 152, 168, 176, 120, 170, 23, 54, 101, 91, 119, 83, 69, 154, 127, 134, 118, 163, 158, 130, 166, 172, 195, 16, 35, 66, 57, 76, 77, 58, 140, 95, 104, 72, 151, 106, 161, 143, 122, 139, 31, 78, 171, 102, 131, 142, 107, 210, 197, 150, 129, 174, 186, 187, 220, 188, 213, 36, 112, 155, 153, 189, 178, 147, 214, 190, 209, 191, 226, 208, 237, 233, 229, 234, 65, 141, 184, 182, 204, 212, 200, 228, 211, 235, 205, 232, 225, 245, 230, 236, 247, 39, 113, 159, 149, 192, 199, 157, 219, 216, 196, 164, 231, 227, 246, 244, 198, 243, 125, 144, 160, 194, 207, 222, 218, 223, 224, 238, 239, 240, 241, 242, 248, 249, 250, 251, 252, 253, 254, 255)
+TIMES = (0, 3, 6, 15, 16, 26, 40, 41, 42, 62, 74, 97, 98, 43, 89, 68, 93, 94, 44, 73, 85, 109, 110, 45, 83, 102, 128, 134, 9, 18, 38, 27, 39, 72, 58, 76, 77, 116, 103, 176, 183, 78, 142, 125, 189, 190, 108, 157, 141, 206, 207, 10, 23, 32, 52, 53, 80, 79, 111, 112, 137, 162, 174, 185, 113, 159, 150, 184, 203, 12, 34, 67, 57, 92, 133, 120, 154, 155, 192, 194, 217, 226, 13, 28, 37, 60, 5, 20, 19, 56, 2, 21, 17, 47, 1, 11, 7, 36, 4, 8, 29, 22, 65, 87, 25, 49, 69, 31, 59, 119, 86, 132, 138, 84, 166, 24, 46, 61, 64, 82, 118, 63, 122, 88, 126, 90, 152, 96, 177, 104, 117, 156, 35, 81, 136, 123, 146, 144, 121, 201, 171, 169, 153, 181, 216, 173, 210, 180, 218, 33, 66, 107, 91, 115, 158, 101, 143, 130, 165, 140, 151, 163, 214, 178, 188, 196, 14, 30, 70, 48, 71, 160, 50, 99, 105, 75, 106, 100, 114, 202, 145, 147, 148, 54, 124, 161, 187, 193, 199, 149, 213, 197, 220, 223, 224, 221, 243, 231, 246, 242, 55, 129, 182, 164, 200, 186, 170, 215, 211, 205, 191, 229, 236, 235, 234, 212, 245, 51, 95, 139, 131, 195, 198, 127, 225, 175, 179, 172, 233, 232, 230, 209, 222, 244, 135, 167, 168, 208, 204, 227, 219, 228, 237, 238, 239, 240, 241, 247, 248, 249, 250, 251, 252, 253)
 F32, BF16 = jnp.float32, jnp.bfloat16
 
 
@@ -245,13 +245,17 @@
         task(functools.partial(do_prep, k, ll, sh, sw), 51, (k,))
     for h in range(2):
         cols = pl.ds(h * HALF, HALF)
-        out = pltpu.make_async_copy(xb.at[:, :, cols], x_out.at[:, :, cols], osem.at[h])
         for s in range(4):
-            task(functools.partial(do_diag, s, h, g, xb, vh, vw, xh, xl), 60 + 4 * h + s, (50, 40 + h, 69 + 4 * h + s))
+            out = pltpu.make_async_copy(xb.at[s, :, cols], x_out.at[s, :, cols], osem.at[h, s])
+
+            def diag(s=s, h=h, out=out):
+                do_diag(s, h, g, xb, vh, vw, xh, xl)
+                out.start()
+
+            task(diag, 60 + 4 * h + s, (50, 40 + h, 69 + 4 * h + s))
+            last(out.wait)
             if s < 3:
                 task(functools.partial(do_stack, s, h, g, xb, sh, sw, xh, xl), 70 + 4 * h + s, (51, 60 + 4 * h + s))
-        task(out.start, None, (63 + 4 * h,))
-        last(out.wait)
 
     for i in arrange(meta, TIMES):
         ops[i]()
@@ -367,7 +371,11 @@
 def do_diag(s, h, g, xb, vh, vw, xh, xl):
     cols = pl.ds(h * HALF, HALF)
     hi, low = split(g[0, :, cols] if s == 0 else xb[s, :, cols])
-    x = dot(vh[s], hi) + (dot(vh[s], low) + dot(vw[s], hi))
+    half = NB // 2
+    a, w = vh[s, :half, :half], vw[s, :half, :half]
+    top = dot(a, hi[:half]) + (dot(a, low[:half]) + dot(w, hi[:half]))
+    a, w = vh[s, half:, :], vw[s, half:, :]
+    x = jnp.concatenate([top, dot(a, hi) + (dot(a, low) + dot(w, hi))], axis=0)
     xb[s, :, cols] = x
     xh[h], xl[h] = split(x)
 
@@ -432,7 +440,7 @@
             vm((2, NB, HALF), BF16), vm((2, NB, HALF), BF16),
             vm((4, NB, NB), F32), vm((16, CW, CW), F32), vm((4, 1, NB), F32),
             dma(()), dma((4, 8, 4)), dma((4, 4)), dma((4, 4)), dma((4, 4, 4)), dma((4, 4, 4)),
-            dma((4, 4)), dma((4, 4)), dma((N_SEND,)), dma((2,)),
+            dma((4, 4)), dma((4, 4)), dma((N_SEND,)), dma((2, 4)),
         ],
         compiler_params=pltpu.CompilerParams(
             collective_id=0, has_side_effects=True, vmem_limit_bytes=66_000_000),

time: 113 us -> 114 us (level)
  no operation moved by 1% of the time
where the time goes in v6:
time: 114 us; the launch traced here: 113 us
  Pallas kernels  112 us (98%)
    pallas_call x1, Pallas kernels, per_device(): pl.pallas_call(gather_kernel, out_shape=(jax.ShapeDtypeStruct((4, NB, wid...  98.8 us
    pallas_call x1, Pallas kernels, per_device(): pl.pallas_call(update_kernel, out_shape=(jax.ShapeDtypeStruct((4, NB, wid...  13.3 us

profile of v6, /device:TPU:0, one launch (start us, length us, event | category | flops | bytes accessed | tf_op | source)
XLA Modules:
  0.0 112.9 jit_solution(14373708857699543284)
XLA Ops:
  0.6 98.8 %gather.1 = (f32[4,512,1024]{2,1,0:T(8,128)}, f32[4,8,64,512]{3,2,1,0:T(8,128)}) custom-call(f32[4,64,512]{2,1,0:T(8,128)} %bitcast.7, f32[512,1024]{1,0:T(8,128)} %bitcast.4), custom_call_target="tpu_custom_call" | custom-call | tf_op jit(solution)/shard_map/gather/pallas_call | solution.py:432
  99.4 13.3 %update.1 = (f32[4,512,1024]{2,1,0:T(8,128)}, f32[512,1024]{1,0:T(8,128)}) custom-call(f32[4,512,1024]{2,1,0:T(8,128)} %get-tuple-element.6.x, f32[4,512,512]{2,1,0:T(8,128)} %bitcast.6, f32[512,1024]{1,0:T(8,128)} %bitcast.5), custom_call_target="tpu_custom_call" | custom-call | tf_op jit(solution)/shard_map/update/pallas_call | solution.py:450

commit v7 on v6

--- a/solution.py
+++ b/solution.py
@@ -15,7 +15,7 @@
 Y_PLUS = (0,)
 E_PLUS = (0,)
 N_SEND = 400
-TIMES = (0, 3, 6, 15, 16, 26, 40, 41, 42, 62, 74, 97, 98, 43, 89, 68, 93, 94, 44, 73, 85, 109, 110, 45, 83, 102, 128, 134, 9, 18, 38, 27, 39, 72, 58, 76, 77, 116, 103, 176, 183, 78, 142, 125, 189, 190, 108, 157, 141, 206, 207, 10, 23, 32, 52, 53, 80, 79, 111, 112, 137, 162, 174, 185, 113, 159, 150, 184, 203, 12, 34, 67, 57, 92, 133, 120, 154, 155, 192, 194, 217, 226, 13, 28, 37, 60, 5, 20, 19, 56, 2, 21, 17, 47, 1, 11, 7, 36, 4, 8, 29, 22, 65, 87, 25, 49, 69, 31, 59, 119, 86, 132, 138, 84, 166, 24, 46, 61, 64, 82, 118, 63, 122, 88, 126, 90, 152, 96, 177, 104, 117, 156, 35, 81, 136, 123, 146, 144, 121, 201, 171, 169, 153, 181, 216, 173, 210, 180, 218, 33, 66, 107, 91, 115, 158, 101, 143, 130, 165, 140, 151, 163, 214, 178, 188, 196, 14, 30, 70, 48, 71, 160, 50, 99, 105, 75, 106, 100, 114, 202, 145, 147, 148, 54, 124, 161, 187, 193, 199, 149, 213, 197, 220, 223, 224, 221, 243, 231, 246, 242, 55, 129, 182, 164, 200, 186, 170, 215, 211, 205, 191, 229, 236, 235, 234, 212, 245, 51, 95, 139, 131, 195, 198, 127, 225, 175, 179, 172, 233, 232, 230, 209, 222, 244, 135, 167, 168, 208, 204, 227, 219, 228, 237, 238, 239, 240, 241, 247, 248, 249, 250, 251, 252, 253)
+TIMES = (0, 6, 9, 14, 22, 28, 34, 44, 45, 63, 59, 110, 115, 46, 70, 71, 99, 105, 47, 79, 80, 100, 109, 48, 85, 86, 114, 124, 7, 17, 37, 24, 38, 68, 62, 87, 88, 117, 135, 162, 169, 89, 132, 138, 183, 193, 90, 133, 148, 180, 181, 3, 8, 12, 18, 30, 56, 50, 92, 93, 146, 173, 201, 206, 94, 156, 165, 202, 203, 11, 29, 74, 40, 75, 136, 98, 126, 137, 185, 179, 215, 221, 1, 15, 13, 42, 4, 25, 26, 43, 2, 19, 21, 53, 5, 33, 32, 55, 10, 27, 64, 52, 128, 41, 49, 103, 96, 84, 67, 175, 167, 82, 123, 97, 217, 20, 51, 73, 60, 111, 108, 61, 145, 116, 121, 81, 177, 152, 168, 176, 120, 170, 23, 54, 101, 91, 119, 83, 69, 154, 127, 134, 118, 163, 158, 130, 166, 172, 195, 16, 35, 66, 57, 76, 77, 58, 140, 95, 104, 72, 151, 106, 161, 143, 122, 139, 31, 78, 171, 102, 131, 142, 107, 210, 197, 150, 129, 174, 186, 187, 220, 188, 213, 36, 112, 155, 153, 189, 178, 147, 214, 190, 209, 191, 226, 208, 237, 233, 229, 234, 65, 141, 184, 182, 204, 212, 200, 228, 211, 235, 205, 232, 225, 245, 230, 236, 247, 39, 113, 159, 149, 192, 199, 157, 219, 216, 196, 164, 231, 227, 246, 244, 198, 243, 125, 144, 160, 194, 207, 222, 218, 223, 224, 238, 239, 240, 241, 248, 249, 250, 251, 252, 253, 254)
 F32, BF16 = jnp.float32, jnp.bfloat16
 
 

time: 114 us -> 111 us (0.974)
  Pallas kernels: 112 us -> 109 us
    pallas_call x1, Pallas kernels: 98.8 us -> 95.9 us  [per_device(): pl.pallas_call(gather_kernel, out_shape=(jax.ShapeDtypeStruct((4, NB, wid...]
where the time goes in v7:
time: 111 us; the launch traced here: 110 us
  Pallas kernels  109 us (98%)
    pallas_call x1, Pallas kernels, per_device(): pl.pallas_call(gather_kernel, out_shape=(jax.ShapeDtypeStruct((4, NB, wid...  95.9 us
    pallas_call x1, Pallas kernels, per_device(): pl.pallas_call(update_kernel, out_shape=(jax.ShapeDtypeStruct((4, NB, wid...  13.3 us

profile of v7, /device:TPU:0, one launch (start us, length us, event | category | flops | bytes accessed | tf_op | source)
XLA Modules:
  0.0 110.1 jit_solution(11286808154732214735)
XLA Ops:
  0.6 95.9 %gather.1 = (f32[4,512,1024]{2,1,0:T(8,128)}, f32[4,8,64,512]{3,2,1,0:T(8,128)}) custom-call(f32[4,64,512]{2,1,0:T(8,128)} %bitcast.7, f32[512,1024]{1,0:T(8,128)} %bitcast.4), custom_call_target="tpu_custom_call" | custom-call | tf_op jit(solution)/shard_map/gather/pallas_call | solution.py:432
  96.6 13.3 %update.1 = (f32[4,512,1024]{2,1,0:T(8,128)}, f32[512,1024]{1,0:T(8,128)}) custom-call(f32[4,512,1024]{2,1,0:T(8,128)} %get-tuple-element.6.x, f32[4,512,512]{2,1,0:T(8,128)} %bitcast.6, f32[512,1024]{1,0:T(8,128)} %bitcast.5), custom_call_target="tpu_custom_call" | custom-call | tf_op jit(solution)/shard_map/update/pallas_call | solution.py:450
